TPU v7x, 32 devices: a whole 2x2x4 slice. The times are simulated.
32 devices in a mesh: gx: 4 (over x, core), gy: 8 (over z, y).
Axes of the slice: x: 2, y: 2, z: 4, core: 2. Of those that a mesh axis runs over, the one named last changes fastest.
Arguments:
- positions: float32 [32, 128, 3, 128], P('gx', 'gy'), may hold values from 0 to 1
- masses: float32 [32, 128, 128], P('gx', 'gy'), may hold values from 0.03 to 0.04
- smoothing: float32 [32, 128, 128], P('gx', 'gy'), may hold values from 0.45 to 0.5
- counts: int32 [32, 128], P('gx', 'gy'), may hold values from 64 to 128, as said below
- pair_list: int32 [32, 128, 8], P('gx', 'gy'), may hold values 0 or 1
- dest: int32 [32, 128], P('gx', 'gy'), may hold values from 0 to 4095, as said below
Outputs:
- moved_state: float32 [32, 128, 5, 128], P('gx', 'gy')
- moved_share: float32 [32, 128], P('gx', 'gy')
Inputs may be any that keep to these rules, and one draw needn't show every extreme that they name: `counts`: tile slots 0 to count - 1 hold particles. `dest`: A permutation of the 4096 slots. A device's block holds slots x in [p * 8, (p + 1) * 8), y in [q * 16, (q + 1) * 16). The tiles of one device that go to one device (itself included) number 0 or exactly 8.
All inputs are finite; a program needn't handle non-finite values. No bound on the sum of `pair_list` on one device may be relied on, other than what follows from the above.
Results may differ from a plain program's by a relative error of at most 0.0003.
Values sent between devices are 32-bit elements; how exact they have to be, the bound alone decides.
A program may use at most 64 MiB of HBM per device.

v0:
```python
import math

import jax
import jax.numpy as jnp
from jax import lax
from jax.sharding import PartitionSpec as P


def extended(block, sides, width):
    for axis, dim in sides:
        count = lax.axis_size(axis)
        forward = [(i, i + 1) for i in range(count - 1)]
        forward.append((count - 1, 0))
        backward = [(target, source) for source, target in forward]
        low = lax.ppermute(
            lax.slice_in_dim(block, block.shape[dim] - width, None, axis=dim), axis, forward
        )
        high = lax.ppermute(lax.slice_in_dim(block, 0, width, axis=dim), axis, backward)
        block = jnp.concatenate([low, block, high], axis=dim)
    return block


def spline(ratio):
    inner_part = 1.0 - 1.5 * ratio * ratio + 0.75 * ratio * ratio * ratio
    remain = jnp.maximum(2.0 - ratio, 0.0)
    outer_part = 0.25 * remain * remain * remain
    return jnp.where(ratio < 1.0, inner_part, outer_part)


def tile_density(pos_self, smooth_self, pos_other, mass_other, step_x, step_y):
    offset = jnp.array([step_x, step_y, 0.0], dtype=jnp.float32)
    delta = pos_other[:, :, None, :] + offset[None, :, None, None] - pos_self[:, :, :, None]
    dist_sq = jnp.sum(delta * delta, axis=1)
    ratio = jnp.sqrt(dist_sq) / smooth_self[:, :, None]
    kernel = spline(ratio) * mass_other[:, None, :]
    return jnp.sum(kernel, axis=2) / (math.pi * smooth_self * smooth_self * smooth_self)


def body(positions, masses, smoothing, counts, pair_list, dest):
    rows_local, cols_local = counts.shape
    slot_width = masses.shape[2]
    grid_x = lax.axis_size("gx")
    grid_y = lax.axis_size("gy")
    device_total = grid_x * grid_y
    tile_total = rows_local * cols_local
    capacity = max(2, 2 * tile_total // device_total)
    slot_ids = jnp.arange(slot_width, dtype=jnp.int32)
    valid_slot = slot_ids[None, None, :] < counts[:, :, None]
    masked = jnp.where(valid_slot, masses, jnp.zeros_like(masses))
    packed = jnp.concatenate([positions, masked[:, :, None, :]], axis=2)
    padded = extended(packed, (("gx", 0), ("gy", 1)), 1)
    weights = pair_list.astype(jnp.float32)

    def row_density(row_index):
        row_block = lax.dynamic_slice_in_dim(padded, row_index, 3, 0)
        own_tile = row_block[1, 1 : cols_local + 1]
        pos_self = own_tile[:, :3]
        smooth_self = lax.dynamic_index_in_dim(smoothing, row_index, 0, keepdims=False)
        weight_row = lax.dynamic_index_in_dim(weights, row_index, 0, keepdims=False)
        summed = jnp.zeros((cols_local, slot_width), jnp.float32)
        offset_index = 0
        for step_x in (-1, 0, 1):
            for step_y in (-1, 0, 1):
                neighbour = row_block[1 + step_x, 1 + step_y : 1 + step_y + cols_local]
                contrib = tile_density(
                    pos_self, smooth_self, neighbour[:, :3], neighbour[:, 3], step_x, step_y
                )
                if step_x == 0 and step_y == 0:
                    summed = summed + contrib
                else:
                    summed = summed + weight_row[:, offset_index][:, None] * contrib
                    offset_index += 1
        return summed

    density = lax.map(row_density, jnp.arange(rows_local, dtype=jnp.int32))
    density = jnp.where(valid_slot, density, jnp.zeros_like(density))
    tile_count = counts.astype(jnp.float32)
    padded_count = jnp.sum((padded[:, :, 3, :] > 0.0).astype(jnp.float32), axis=-1)
    neighbour_sum = jnp.zeros((rows_local, cols_local), jnp.float32)
    offset_index = 0
    for step_x in (-1, 0, 1):
        for step_y in (-1, 0, 1):
            if step_x == 0 and step_y == 0:
                continue
            beside = padded_count[
                1 + step_x : 1 + step_x + rows_local, 1 + step_y : 1 + step_y + cols_local
            ]
            neighbour_sum = neighbour_sum + weights[:, :, offset_index] * beside
            offset_index += 1
    pair_work = tile_count * (tile_count + neighbour_sum)
    total_work = lax.psum(jnp.sum(pair_work), ("gx", "gy"))
    work_share = pair_work * float(tile_total * device_total) / total_work
    row_span = cols_local * grid_y
    slot_x = dest // row_span
    slot_y = dest % row_span
    target = (slot_x // rows_local * grid_y + slot_y // cols_local).reshape(-1)
    slot_local = (slot_x % rows_local * cols_local + slot_y % cols_local).reshape(-1)
    tile_order = jnp.arange(tile_total, dtype=jnp.int32)
    same_target = target[:, None] == target[None, :]
    earlier = tile_order[None, :] < tile_order[:, None]
    rank_slot = jnp.sum(jnp.logical_and(same_target, earlier).astype(jnp.int32), axis=1)
    send_index = target * capacity + rank_slot
    tile_state = jnp.concatenate([positions, masked[:, :, None, :], density[:, :, None, :]], axis=2)
    tile_state = tile_state.reshape(tile_total, 5, slot_width)
    send_state = (
        jnp.zeros((device_total * capacity, 5, slot_width), jnp.float32)
        .at[send_index]
        .set(tile_state)
    )
    send_share = (
        jnp.zeros((device_total * capacity,), jnp.float32)
        .at[send_index]
        .set(work_share.reshape(-1))
    )
    send_slot = (
        jnp.full((device_total * capacity,), -1.0, jnp.float32)
        .at[send_index]
        .set(slot_local.astype(jnp.float32))
    )
    received = (
        lax.all_to_all(
            send_state.reshape(device_total, capacity, 5, slot_width),
            ("gx", "gy"),
            split_axis=0,
            concat_axis=0,
            tiled=True,
        ),
        lax.all_to_all(
            send_share.reshape(device_total, capacity),
            ("gx", "gy"),
            split_axis=0,
            concat_axis=0,
            tiled=True,
        ),
        lax.all_to_all(
            send_slot.reshape(device_total, capacity),
            ("gx", "gy"),
            split_axis=0,
            concat_axis=0,
            tiled=True,
        ),
    )
    recv_state = received[0].reshape(device_total * capacity, 5, slot_width)
    recv_share = received[1].reshape(-1)
    recv_slot = received[2].reshape(-1).astype(jnp.int32)
    place_index = jnp.where(recv_slot >= 0, recv_slot, tile_total)
    moved_state = (
        jnp.zeros((tile_total, 5, slot_width), jnp.float32)
        .at[place_index]
        .set(recv_state, mode="drop")
    )
    moved_share = jnp.zeros((tile_total,), jnp.float32).at[place_index].set(recv_share, mode="drop")
    return (
        moved_state.reshape(rows_local, cols_local, 5, slot_width),
        moved_share.reshape(rows_local, cols_local),
    )


def solution(mesh):
    in_specs = (
        P("gx", "gy", None, None),
        P("gx", "gy", None),
        P("gx", "gy", None),
        P("gx", "gy"),
        P("gx", "gy", None),
        P("gx", "gy"),
    )
    out_specs = (P("gx", "gy", None, None), P("gx", "gy"))
    return jax.shard_map(body, mesh=mesh, in_specs=in_specs, out_specs=out_specs, check_vma=False)
```

profile of v0, /device:TPU:0, one launch (start us, length us, event | category | flops | bytes accessed | tf_op | source)
XLA Modules:
  0.0 322.3 jit_solution(7267880137546761152)
XLA Ops:
  7.8 6.6 %all-to-all-start = ((f32[32,1,8]{2,1,0:T(1,128)}), f32[32,1,8]{2,1,0:T(1,128)S(1)}, u32[]{:S(2)}, u32[]{:S(2)}) async-start(f32[32,1,8]{2,1,0:T(1,128)} %bitcast.2), calls=%async_computation | async-start | bytes 32768 | tf_op jit(solution)/shard_map/all_to_all | solution.py:135
  25.5 40.5 %psum.7 = f32[]{:T(128)} all-reduce(f32[]{:T(128)} %get-tuple-element.193), channel_id=1, replica_groups=mesh['gx'=4,'gy'=8] {'gx','gy'}, use_global_device_ids=true, to_apply=%region_26.27 | all-reduce | flops 1 | bytes 8 | tf_op jit(solution)/shard_map/psum | solution.py:91
  66.6 207.6 %while.12 = (s32[]{:T(128)}, f32[8,16,128]{2,1,0:T(8,128)}, s32[8]{0:T(128)}, f32[8,16,8]{1,0,2:T(8,128)S(1)}, f32[10,18,4,128]{3,1,2,0:T(8,128)}, /*index=5*/f3...) while((s32[]{:T(128)}, f32[8,16,128]{2,1,0:T(8,128)}, ...), condition=%wide.region_21.22_spmd.clone.clone, body=%wide.region_2.21_spmd.sunk.clone.sunk.clone | while | flops 59070472 | bytes 20983164 | solution.py:75
  72.5 7.4 %multiply_reduce_fusion.11 = (f32[16,128,128]{2,1,0:T(8,128)S(1)}, f32[16,128,128]{2,1,0:T(8,128)S(1)}, f32[16,128,128]{2,1,0:T(8,128)S(1)}, f32[16,128,128]{2,1...) fusion(f32[16,3,128]{2,1,0:T(4,128)S(1)} %copy.107, ...), kind=kLoop, calls=%fused_computation.13.clone.1.clone | loop fusion | flops 18874368 | bytes 9658368 | tf_op jit(solution)/shard_map/while/body/eval_jaxpr/reduce_sum | solution.py:33
  81.8 9.4 %fusion.97 = (f32[16,128]{1,0:T(8,128)S(1)}, f32[16,128]{1,0:T(8,128)S(1)}, f32[16,128]{1,0:T(8,128)S(1)}, f32[16,128]{1,0:T(8,128)S(1)}, f32[16,128]{1,0:T(8,12...) fusion(f32[16,128,128]{2,1,0:T(8,128)S(1)} %get-tuple-element.4, ...), kind=kLoop, calls=%fused_computation.45.clone.1.clone | loop fusion | flops 40089600 | bytes 9592832 | tf_op jit(solution)/shard_map/while/body/eval_jaxpr/reduce_sum | solution.py:36
  98.5 7.4 %multiply_reduce_fusion.11 = (f32[16,128,128]{2,1,0:T(8,128)S(1)}, f32[16,128,128]{2,1,0:T(8,128)S(1)}, f32[16,128,128]{2,1,0:T(8,128)S(1)}, f32[16,128,128]{2,1...) fusion(f32[16,3,128]{2,1,0:T(4,128)S(1)} %copy.107, ...), kind=kLoop, calls=%fused_computation.13.clone.1.clone | loop fusion | flops 18874368 | bytes 9658368 | tf_op jit(solution)/shard_map/while/body/eval_jaxpr/reduce_sum | solution.py:33
  107.8 9.4 %fusion.97 = (f32[16,128]{1,0:T(8,128)S(1)}, f32[16,128]{1,0:T(8,128)S(1)}, f32[16,128]{1,0:T(8,128)S(1)}, f32[16,128]{1,0:T(8,128)S(1)}, f32[16,128]{1,0:T(8,12...) fusion(f32[16,128,128]{2,1,0:T(8,128)S(1)} %get-tuple-element.4, ...), kind=kLoop, calls=%fused_computation.45.clone.1.clone | loop fusion | flops 40089600 | bytes 9592832 | tf_op jit(solution)/shard_map/while/body/eval_jaxpr/reduce_sum | solution.py:36
  124.5 7.4 %multiply_reduce_fusion.11 = (f32[16,128,128]{2,1,0:T(8,128)S(1)}, f32[16,128,128]{2,1,0:T(8,128)S(1)}, f32[16,128,128]{2,1,0:T(8,128)S(1)}, f32[16,128,128]{2,1...) fusion(f32[16,3,128]{2,1,0:T(4,128)S(1)} %copy.107, ...), kind=kLoop, calls=%fused_computation.13.clone.1.clone | loop fusion | flops 18874368 | bytes 9658368 | tf_op jit(solution)/shard_map/while/body/eval_jaxpr/reduce_sum | solution.py:33
  133.7 9.4 %fusion.97 = (f32[16,128]{1,0:T(8,128)S(1)}, f32[16,128]{1,0:T(8,128)S(1)}, f32[16,128]{1,0:T(8,128)S(1)}, f32[16,128]{1,0:T(8,128)S(1)}, f32[16,128]{1,0:T(8,12...) fusion(f32[16,128,128]{2,1,0:T(8,128)S(1)} %get-tuple-element.4, ...), kind=kLoop, calls=%fused_computation.45.clone.1.clone | loop fusion | flops 40089600 | bytes 9592832 | tf_op jit(solution)/shard_map/while/body/eval_jaxpr/reduce_sum | solution.py:36
  150.4 7.4 %multiply_reduce_fusion.11 = (f32[16,128,128]{2,1,0:T(8,128)S(1)}, f32[16,128,128]{2,1,0:T(8,128)S(1)}, f32[16,128,128]{2,1,0:T(8,128)S(1)}, f32[16,128,128]{2,1...) fusion(f32[16,3,128]{2,1,0:T(4,128)S(1)} %copy.107, ...), kind=kLoop, calls=%fused_computation.13.clone.1.clone | loop fusion | flops 18874368 | bytes 9658368 | tf_op jit(solution)/shard_map/while/body/eval_jaxpr/reduce_sum | solution.py:33
  159.7 9.4 %fusion.97 = (f32[16,128]{1,0:T(8,128)S(1)}, f32[16,128]{1,0:T(8,128)S(1)}, f32[16,128]{1,0:T(8,128)S(1)}, f32[16,128]{1,0:T(8,128)S(1)}, f32[16,128]{1,0:T(8,12...) fusion(f32[16,128,128]{2,1,0:T(8,128)S(1)} %get-tuple-element.4, ...), kind=kLoop, calls=%fused_computation.45.clone.1.clone | loop fusion | flops 40089600 | bytes 9592832 | tf_op jit(solution)/shard_map/while/body/eval_jaxpr/reduce_sum | solution.py:36
  176.3 7.4 %multiply_reduce_fusion.11 = (f32[16,128,128]{2,1,0:T(8,128)S(1)}, f32[16,128,128]{2,1,0:T(8,128)S(1)}, f32[16,128,128]{2,1,0:T(8,128)S(1)}, f32[16,128,128]{2,1...) fusion(f32[16,3,128]{2,1,0:T(4,128)S(1)} %copy.107, ...), kind=kLoop, calls=%fused_computation.13.clone.1.clone | loop fusion | flops 18874368 | bytes 9658368 | tf_op jit(solution)/shard_map/while/body/eval_jaxpr/reduce_sum | solution.py:33
  185.6 9.4 %fusion.97 = (f32[16,128]{1,0:T(8,128)S(1)}, f32[16,128]{1,0:T(8,128)S(1)}, f32[16,128]{1,0:T(8,128)S(1)}, f32[16,128]{1,0:T(8,128)S(1)}, f32[16,128]{1,0:T(8,12...) fusion(f32[16,128,128]{2,1,0:T(8,128)S(1)} %get-tuple-element.4, ...), kind=kLoop, calls=%fused_computation.45.clone.1.clone | loop fusion | flops 40089600 | bytes 9592832 | tf_op jit(solution)/shard_map/while/body/eval_jaxpr/reduce_sum | solution.py:36
  202.3 7.4 %multiply_reduce_fusion.11 = (f32[16,128,128]{2,1,0:T(8,128)S(1)}, f32[16,128,128]{2,1,0:T(8,128)S(1)}, f32[16,128,128]{2,1,0:T(8,128)S(1)}, f32[16,128,128]{2,1...) fusion(f32[16,3,128]{2,1,0:T(4,128)S(1)} %copy.107, ...), kind=kLoop, calls=%fused_computation.13.clone.1.clone | loop fusion | flops 18874368 | bytes 9658368 | tf_op jit(solution)/shard_map/while/body/eval_jaxpr/reduce_sum | solution.py:33
  211.5 9.4 %fusion.97 = (f32[16,128]{1,0:T(8,128)S(1)}, f32[16,128]{1,0:T(8,128)S(1)}, f32[16,128]{1,0:T(8,128)S(1)}, f32[16,128]{1,0:T(8,128)S(1)}, f32[16,128]{1,0:T(8,12...) fusion(f32[16,128,128]{2,1,0:T(8,128)S(1)} %get-tuple-element.4, ...), kind=kLoop, calls=%fused_computation.45.clone.1.clone | loop fusion | flops 40089600 | bytes 9592832 | tf_op jit(solution)/shard_map/while/body/eval_jaxpr/reduce_sum | solution.py:36
  228.3 7.4 %multiply_reduce_fusion.11 = (f32[16,128,128]{2,1,0:T(8,128)S(1)}, f32[16,128,128]{2,1,0:T(8,128)S(1)}, f32[16,128,128]{2,1,0:T(8,128)S(1)}, f32[16,128,128]{2,1...) fusion(f32[16,3,128]{2,1,0:T(4,128)S(1)} %copy.107, ...), kind=kLoop, calls=%fused_computation.13.clone.1.clone | loop fusion | flops 18874368 | bytes 9658368 | tf_op jit(solution)/shard_map/while/body/eval_jaxpr/reduce_sum | solution.py:33
  237.5 9.4 %fusion.97 = (f32[16,128]{1,0:T(8,128)S(1)}, f32[16,128]{1,0:T(8,128)S(1)}, f32[16,128]{1,0:T(8,128)S(1)}, f32[16,128]{1,0:T(8,128)S(1)}, f32[16,128]{1,0:T(8,12...) fusion(f32[16,128,128]{2,1,0:T(8,128)S(1)} %get-tuple-element.4, ...), kind=kLoop, calls=%fused_computation.45.clone.1.clone | loop fusion | flops 40089600 | bytes 9592832 | tf_op jit(solution)/shard_map/while/body/eval_jaxpr/reduce_sum | solution.py:36
  254.2 7.4 %multiply_reduce_fusion.11 = (f32[16,128,128]{2,1,0:T(8,128)S(1)}, f32[16,128,128]{2,1,0:T(8,128)S(1)}, f32[16,128,128]{2,1,0:T(8,128)S(1)}, f32[16,128,128]{2,1...) fusion(f32[16,3,128]{2,1,0:T(4,128)S(1)} %copy.107, ...), kind=kLoop, calls=%fused_computation.13.clone.1.clone | loop fusion | flops 18874368 | bytes 9658368 | tf_op jit(solution)/shard_map/while/body/eval_jaxpr/reduce_sum | solution.py:33
  263.5 9.4 %fusion.97 = (f32[16,128]{1,0:T(8,128)S(1)}, f32[16,128]{1,0:T(8,128)S(1)}, f32[16,128]{1,0:T(8,128)S(1)}, f32[16,128]{1,0:T(8,128)S(1)}, f32[16,128]{1,0:T(8,12...) fusion(f32[16,128,128]{2,1,0:T(8,128)S(1)} %get-tuple-element.4, ...), kind=kLoop, calls=%fused_computation.45.clone.1.clone | loop fusion | flops 40089600 | bytes 9592832 | tf_op jit(solution)/shard_map/while/body/eval_jaxpr/reduce_sum | solution.py:36
  277.7 5.2 %all-to-all-start.2 = ((f32[32,1,8]{2,1,0:T(1,128)}), f32[32,1,8]{2,1,0:T(1,128)S(1)}, u32[]{:S(2)}, u32[]{:S(2)}) async-start(f32[32,1,8]{2,1,0:T(1,128)} %bitcast.20), calls=%async_computation.2 | async-start | bytes 32768 | tf_op jit(solution)/shard_map/all_to_all | solution.py:128
  283.6 4.3 %scatter_fusion = f32[256,5,128]{2,1,0:T(8,128)S(1)} fusion(f32[256,5,128]{2,1,0:T(8,128)S(1)} %broadcast_in_dim.19, s32[128]{0:T(128)S(1)} %copy-done.8, f32[128,5,128]{2,1,0:T(8,128)S(1)} %copy.76), kind=kCustom, calls=%fused_computation.1 | custom fusion | bytes 983552 | tf_op jit(solution)/shard_map/scatter | solution.py:108
  290.0 4.7 %all-to-all-start.1 = ((f32[32,8,5,128]{3,1,2,0:T(8,128)}), f32[32,8,5,128]{3,1,2,0:T(8,128)S(1)}, u32[]{:S(2)}, u32[]{:S(2)}) async-start(f32[32,8,5,128]{3,1,2,0:T(8,128)} %copy.77), calls=%async_computation.1 | async-start | bytes 1310720 | tf_op jit(solution)/shard_map/all_to_all | solution.py:121
  298.3 15.5 %all-to-all-done.1 = f32[32,8,5,128]{3,1,2,0:T(8,128)S(1)} async-done(((f32[32,8,5,128]{3,1,2,0:T(8,128)}), f32[32,8,5,128]{3,1,2,0:T(8,128)S(1)}, u32[]{:S(2)}, u32[]{:S(2)}) %all-to-all-start.1) | async-done | bytes 655392 | tf_op jit(solution)/shard_map/all_to_all | solution.py:121
  314.3 7.3 %scatter_fusion.1 = f32[128,5,128]{2,1,0:T(8,128)S(1)} fusion(f32[128,5,128]{2,1,0:T(8,128)S(1)} %broadcast_in_dim.16, s32[256]{0:T(256)S(1)} %bitcast.252, f32[256,5,128]{2,1,0:T(8,128)S(1)} %copy.79), kind=kCustom, calls=%fused_computation.2 | custom fusion | bytes 1967104 | tf_op jit(solution)/shard_map/scatter | solution.py:150
  (268 shorter events, 79.7 us)
Async XLA Ops:
  0.6 20.5 %copy-start = (f32[8,16,3,128]{3,1,2,0:T(8,128)S(1)}, f32[8,16,3,128]{3,1,2,0:T(8,128)}, u32[]{:S(2)}) copy-start(f32[8,16,3,128]{3,1,2,0:T(8,128)} %param.17) | copy-start | bytes 589828
  0.6 20.5 %copy-start.2 = (s32[8,16,8]{1,2,0:T(8,128)S(1)}, s32[8,16,8]{1,2,0:T(8,128)}, u32[]{:S(2)}) copy-start(s32[8,16,8]{1,2,0:T(8,128)} %param.21) | copy-start | bytes 12292
  2.4 22.4 %copy-start.1 = (s32[8,16]{1,0:T(8,128)S(1)}, s32[8,16]{1,0:T(8,128)}, u32[]{:S(2)}) copy-start(s32[8,16]{1,0:T(8,128)} %param.20) | copy-start | bytes 1540
  2.4 12.9 %collective-permute-start = (f32[1,16,4,128]{3,1,2,0:T(8,128)S(1)}, f32[1,16,4,128]{3,1,2,0:T(8,128)S(1)}, u32[]{:S(2)}, u32[]{:S(2)}) collective-permute-start(f32[1,16,4,128]{3,1,2,0:T(8,128)S(1)} %get-tuple-element.232), channel_id=1, source_target_pairs={{0,8},{8,16},{16,24},{24,0},{1,9},{9,17},{17,25},{25,1},{2,10},{10... | collective-permute-start | bytes 98312 | tf_op jit(solution)/shard_map/ppermute | solution.py:15
  2.9 12.4 %collective-permute-start.1 = (f32[1,16,4,128]{3,1,2,0:T(8,128)S(1)}, f32[1,16,4,128]{3,1,2,0:T(8,128)S(1)}, u32[]{:S(2)}, u32[]{:S(2)}) collective-permute-start(f32[1,16,4,128]{3,1,2,0:T(8,128)S(1)} %get-tuple-element.233), channel_id=1, source_target_pairs={{8,0},{16,8},{24,16},{0,24},{9,1},{17,9},{25,17},{1,25},{10,2},{18... | collective-permute-start | bytes 98312 | tf_op jit(solution)/shard_map/ppermute | solution.py:18
  6.0 60.6 %copy-start.3 = (f32[3]{0:T(128)S(1)}, f32[3]{0:T(128)}, u32[]{:S(2)}) copy-start(f32[3]{0:T(128)} %constant.140.clone..sunk.2) | copy-start | bytes 40
  6.0 60.6 %copy-start.4 = (f32[3]{0:T(128)S(1)}, f32[3]{0:T(128)}, u32[]{:S(2)}) copy-start(f32[3]{0:T(128)} %constant.141.clone..sunk.2) | copy-start | bytes 40
  6.0 60.6 %copy-start.5 = (f32[3]{0:T(128)S(1)}, f32[3]{0:T(128)}, u32[]{:S(2)}) copy-start(f32[3]{0:T(128)} %constant.142.clone..sunk.2) | copy-start | bytes 40
  6.1 60.6 %copy-start.6 = (f32[3]{0:T(128)S(1)}, f32[3]{0:T(128)}, u32[]{:S(2)}) copy-start(f32[3]{0:T(128)} %constant.143.clone..sunk.2) | copy-start | bytes 40
  6.1 1.7 copy-start.7
  7.8 269.9 %all-to-all-start = ((f32[32,1,8]{2,1,0:T(1,128)}), f32[32,1,8]{2,1,0:T(1,128)S(1)}, u32[]{:S(2)}, u32[]{:S(2)}) async-start(f32[32,1,8]{2,1,0:T(1,128)} %bitcast.2), calls=%async_computation | async-start | bytes 32768 | tf_op jit(solution)/shard_map/all_to_all | solution.py:135
  16.3 6.5 %collective-permute-start.2 = (f32[10,1,4,128]{3,1,2,0:T(1,128)S(1)}, f32[10,1,4,128]{3,1,2,0:T(1,128)S(1)}, u32[]{:S(2)}, u32[]{:S(2)}) collective-permute-start(f32[10,1,4,128]{3,1,2,0:T(1,128)S(1)} %get-tuple-element.230), channel_id=1, source_target_pairs={{0,1},{1,2},{2,3},{3,4},{4,5},{5,6},{6,7},{7,0},{8,9},{9,10},{10,1... | collective-permute-start | bytes 61448 | tf_op jit(solution)/shard_map/ppermute | solution.py:15
  18.1 4.7 %collective-permute-start.3 = (f32[10,1,4,128]{3,1,2,0:T(1,128)S(1)}, f32[10,1,4,128]{3,1,2,0:T(1,128)S(1)}, u32[]{:S(2)}, u32[]{:S(2)}) collective-permute-start(f32[10,1,4,128]{3,1,2,0:T(1,128)S(1)} %get-tuple-element.231), channel_id=1, source_target_pairs={{1,0},{2,1},{3,2},{4,3},{5,4},{6,5},{7,6},{0,7},{9,8},{10,9},{11,1... | collective-permute-start | bytes 61448 | tf_op jit(solution)/shard_map/ppermute | solution.py:18
  277.7 12.3 %all-to-all-start.2 = ((f32[32,1,8]{2,1,0:T(1,128)}), f32[32,1,8]{2,1,0:T(1,128)S(1)}, u32[]{:S(2)}, u32[]{:S(2)}) async-start(f32[32,1,8]{2,1,0:T(1,128)} %bitcast.20), calls=%async_computation.2 | async-start | bytes 32768 | tf_op jit(solution)/shard_map/all_to_all | solution.py:128
  283.0 0.7 copy-start.8
  290.0 23.8 %all-to-all-start.1 = ((f32[32,8,5,128]{3,1,2,0:T(8,128)}), f32[32,8,5,128]{3,1,2,0:T(8,128)S(1)}, u32[]{:S(2)}, u32[]{:S(2)}) async-start(f32[32,8,5,128]{3,1,2,0:T(8,128)} %copy.77), calls=%async_computation.1 | async-start | bytes 1310720 | tf_op jit(solution)/shard_map/all_to_all | solution.py:121
where the time goes:
time: 325 us; the launch traced here: 322 us
  other arithmetic  168 us (52%)
  local copies, waits for them, and re-layouts  47.3 us (15%)
  blocking collectives  40.5 us (12%)
  starting transfers between devices  23.8 us (7%)
  loops' own time  23.3 us (7%)
  waiting for transfers between devices  18.3 us (6%)
    reduce_sum x8, other arithmetic, tile_density(): jnp.sum(kernel, axis=2)  74.9 us
    reduce_sum x8, other arithmetic, tile_density(): dist_sq = jnp.sum(delta * delta, axis=1)  59.4 us
    psum x1, blocking collectives, body(): total_work = lax.psum(jnp.sum(pair_work), ('gx', 'gy'))  40.5 us
    another operation x1, loops' own time, body(): density = lax.map(row_density, jnp.arange(rows_local, dtype=jnp.int32))  23.3 us
    all_to_all x1, waiting for transfers between devices, body(): lax.all_to_all(send_state.reshape(device_total, capacity, 5, slot_width),...  15.5 us
    add x32, other arithmetic, tile_density(): pos_other[:, :, None, :] + offset[None, :, None, None]  13.2 us
    dynamic_update_slice x8, other arithmetic, body(): density = lax.map(row_density, jnp.arange(rows_local, dtype=jnp.int32))  11.1 us
    dynamic_slice x8, local copies, waits for them, and re-layouts, body(): density = lax.map(row_density, jnp.arange(rows_local, dtype=jnp.int32))  10.1 us
  transfers between devices with their start and end apart: 7, of which 3 were waited for; matrix products, arithmetic and copies ran while one was open for 63% of the time, Pallas kernels for 0%

commit v1 on v0

v1 whole, which is shorter than its diff:
```python
import functools
import math

import jax
import jax.numpy as jnp
from jax import lax
from jax.experimental import pallas as pl
from jax.experimental.pallas import tpu as pltpu
from jax.sharding import PartitionSpec as P

OFFSETS = tuple((a, b) for a in (-1, 0, 1) for b in (-1, 0, 1) if (a, b) != (0, 0))
UNROLL = 4


def extended(block, sides, width):
    for axis, dim in sides:
        count = lax.axis_size(axis)
        forward = [(i, i + 1) for i in range(count - 1)]
        forward.append((count - 1, 0))
        backward = [(target, source) for source, target in forward]
        low = lax.ppermute(
            lax.slice_in_dim(block, block.shape[dim] - width, None, axis=dim), axis, forward
        )
        high = lax.ppermute(lax.slice_in_dim(block, 0, width, axis=dim), axis, backward)
        block = jnp.concatenate([low, block, high], axis=dim)
    return block


def list_kernel(rows, cols, pair_ref, list_ref, count_ref):
    wide = cols + 2
    dummy = (rows + 2) * wide

    def tile(t, ptr):
        tx, ty = t // cols, lax.rem(t, cols)
        base = (tx + 1) * wide + ty + 1
        list_ref[ptr] = (base << 16) | (t << 4) | 4
        ptr = ptr + 1
        for k, (a, b) in enumerate(OFFSETS):
            code = (a + 1) * 3 + (b + 1)
            list_ref[ptr] = ((base + a * wide + b) << 16) | (t << 4) | code
            ptr = ptr + jnp.where(pair_ref[t * 8 + k] != 0, 1, 0)
        return ptr

    ptr = lax.fori_loop(0, rows * cols, tile, jnp.int32(0))
    for u in range(UNROLL):
        list_ref[ptr + u] = dummy << 16
    count_ref[0] = (ptr + UNROLL - 1) // UNROLL


def split3(value):
    high = value.astype(jnp.bfloat16).astype(jnp.float32)
    rest = value - high
    mid = rest.astype(jnp.bfloat16).astype(jnp.float32)
    return high, mid, rest - mid


def density_kernel(
    tiles, sources, list_ref, count_ref, send_ref, feat_ref, own_ref, norm_ref,
    out_ref, lhs_ref, mass_ref, acc_ref
):
    width = norm_ref.shape[1]

    def prep(s, carry):
        feat = feat_ref[s]
        high, mid, low = split3(feat)
        block = jnp.concatenate([high, high, mid, mid, high, low, feat], axis=0)
        turned = block.T
        lhs_ref[s] = turned[:, :48].astype(jnp.bfloat16)
        mass_ref[s] = jnp.broadcast_to(turned[:, 53:54], (width, width))
        return carry

    lax.fori_loop(0, sources, prep, 0, unroll=2)
    lhs_ref[sources] = jnp.zeros((width, 48), jnp.bfloat16)
    mass_ref[sources] = jnp.zeros((width, width), jnp.float32)
    acc_ref[...] = jnp.zeros_like(acc_ref)
    out_ref[...] = jnp.zeros_like(out_ref)

    def step(i, carry):
        parts = []
        for u in range(UNROLL):
            entry = list_ref[i * UNROLL + u]
            source = entry >> 16
            t = (entry >> 4) & 4095
            code = entry & 15
            a = code // 3 - 1
            b = lax.rem(code, 3) - 1
            off_x = a.astype(jnp.float32)
            off_y = b.astype(jnp.float32)
            off_sq = (a * a + b * b).astype(jnp.float32)
            own = own_ref[t]
            form = own[0:8] + off_x * own[8:16] + off_y * own[16:24] + off_sq * own[24:32]
            high, mid, low = split3(form)
            rhs = jnp.concatenate([high, mid, high, mid, low, high], axis=0).astype(jnp.bfloat16)
            sq = jnp.dot(lhs_ref[source], rhs, preferred_element_type=jnp.float32)
            sq = jnp.maximum(sq, 1e-20)
            ratio = sq * lax.rsqrt(sq)
            outer = jnp.maximum(2.0 - ratio, 0.0)
            inner = jnp.maximum(1.0 - ratio, 0.0)
            value = (outer * outer * outer - 4.0 * (inner * inner * inner)) * mass_ref[source]
            parts.append((t, jnp.sum(value.reshape(width // 8, 8, width), axis=0)))
        for t, part in parts:
            acc_ref[t] += part
        return carry

    lax.fori_loop(0, count_ref[0], step, 0)

    def finish(t, carry):
        total = jnp.sum(acc_ref[t], axis=0, keepdims=True)
        out_ref[pl.ds(send_ref[t], 1), :] = total * norm_ref[pl.ds(t, 1), :]
        return carry

    lax.fori_loop(0, tiles, finish, 0, unroll=4)


def place_kernel(tiles, from_ref, state_ref, dens_ref, out_ref):
    def put(s, carry):
        row = from_ref[s]
        out_ref[s, 0:4, :] = state_ref[row, 0:4, :]
        out_ref[s, 4:5, :] = dens_ref[pl.ds(row, 1), :]
        return carry

    lax.fori_loop(0, tiles, put, 0, unroll=8)


SMEM = pl.BlockSpec(memory_space=pltpu.SMEM)
VMEM = pl.BlockSpec(memory_space=pltpu.VMEM)


def body(positions, masses, smoothing, counts, pair_list, dest):
    rows_local, cols_local = counts.shape
    slot_width = masses.shape[2]
    grid_x = lax.axis_size("gx")
    grid_y = lax.axis_size("gy")
    device_total = grid_x * grid_y
    tile_total = rows_local * cols_local
    capacity = max(2, 2 * tile_total // device_total)
    send_rows = device_total * capacity
    slot_ids = jnp.arange(slot_width, dtype=jnp.int32)
    valid_slot = slot_ids[None, None, :] < counts[:, :, None]
    masked = jnp.where(valid_slot, masses, jnp.zeros_like(masses))
    packed = jnp.concatenate([positions, masked[:, :, None, :]], axis=2)
    padded = extended(packed, (("gx", 0), ("gy", 1)), 1)
    weights = pair_list.astype(jnp.float32)

    list_size = 9 * tile_total + 2 * UNROLL
    pair_entries, pair_groups = pl.pallas_call(
        functools.partial(list_kernel, rows_local, cols_local),
        out_shape=(
            jax.ShapeDtypeStruct((list_size,), jnp.int32),
            jax.ShapeDtypeStruct((1,), jnp.int32),
        ),
        in_specs=[SMEM],
        out_specs=(SMEM, SMEM),
        cost_estimate=pl.CostEstimate(flops=4000000, bytes_accessed=8192, transcendentals=0),
        name="pair_entries",
    )(pair_list.reshape(-1))

    centred = (positions - 0.5).reshape(tile_total, 3, slot_width)
    smooth = smoothing.reshape(tile_total, 1, slot_width)
    inv_sq = 1.0 / (smooth * smooth)
    own_x, own_y, own_z = centred[:, 0:1], centred[:, 1:2], centred[:, 2:3]
    own_sq = own_x * own_x + own_y * own_y + own_z * own_z
    zero = jnp.zeros_like(inv_sq)
    own_form = jnp.concatenate(
        [-2.0 * inv_sq * own_x, -2.0 * inv_sq * own_y, -2.0 * inv_sq * own_z, inv_sq, inv_sq * own_sq,
         zero, zero, zero,
         2.0 * inv_sq, zero, zero, zero, -2.0 * inv_sq * own_x, zero, zero, zero,
         zero, 2.0 * inv_sq, zero, zero, -2.0 * inv_sq * own_y, zero, zero, zero,
         zero, zero, zero, zero, inv_sq, zero, zero, zero],
        axis=1,
    )
    norm = jnp.where(valid_slot, 0.25 / (math.pi * smoothing * smoothing * smoothing), 0.0)
    norm = norm.reshape(tile_total, slot_width)

    row_span = cols_local * grid_y
    slot_x = dest // row_span
    slot_y = dest % row_span
    target = (slot_x // rows_local * grid_y + slot_y // cols_local).reshape(-1)
    slot_local = (slot_x % rows_local * cols_local + slot_y % cols_local).reshape(-1)
    tile_order = jnp.arange(tile_total, dtype=jnp.int32)
    same_target = target[:, None] == target[None, :]
    earlier = tile_order[None, :] < tile_order[:, None]
    rank_slot = jnp.sum(jnp.logical_and(same_target, earlier).astype(jnp.int32), axis=1)
    send_index = target * capacity + rank_slot

    tile_count = counts.astype(jnp.float32)
    padded_count = jnp.sum((padded[:, :, 3, :] > 0.0).astype(jnp.float32), axis=-1)
    neighbour_sum = jnp.zeros((rows_local, cols_local), jnp.float32)
    for k, (a, b) in enumerate(OFFSETS):
        beside = padded_count[1 + a : 1 + a + rows_local, 1 + b : 1 + b + cols_local]
        neighbour_sum = neighbour_sum + weights[:, :, k] * beside
    pair_work = tile_count * (tile_count + neighbour_sum)
    local_work = jnp.sum(pair_work)

    lane = slot_ids[None, :]
    note = jnp.where(lane == 0, pair_work.reshape(-1, 1), 0.0)
    note = jnp.where(lane == 1, (slot_local + 1).astype(jnp.float32)[:, None], note)
    tile_state = jnp.concatenate(
        [packed.reshape(tile_total, 4, slot_width), note[:, None, :]], axis=1
    )
    send_state = jnp.zeros((send_rows, 5, slot_width), jnp.float32).at[send_index].set(tile_state)
    mark = jnp.logical_and(jnp.arange(5)[:, None] == 4, lane == 2)
    send_state = jnp.where(mark[None], local_work, send_state)
    recv_state = lax.all_to_all(
        send_state.reshape(device_total, capacity, 5, slot_width),
        ("gx", "gy"),
        split_axis=0,
        concat_axis=0,
        tiled=True,
    ).reshape(send_rows, 5, slot_width)

    sources = (rows_local + 2) * (cols_local + 2)
    halo = padded.reshape(sources, 4, slot_width)
    halo_pos = halo[:, :3] - 0.5
    halo_sq = jnp.sum(halo_pos * halo_pos, axis=1, keepdims=True)
    halo_one = jnp.ones_like(halo_sq)
    features = jnp.concatenate(
        [halo_pos, halo_sq, halo_one, halo[:, 3:4], 0.0 * halo_one, 0.0 * halo_one], axis=1
    )
    send_density = pl.pallas_call(
        functools.partial(density_kernel, tile_total, sources),
        out_shape=jax.ShapeDtypeStruct((send_rows, slot_width), jnp.float32),
        in_specs=[SMEM, SMEM, SMEM, VMEM, VMEM, VMEM],
        out_specs=VMEM,
        scratch_shapes=[
            pltpu.VMEM((sources + 1, slot_width, 48), jnp.bfloat16),
            pltpu.VMEM((sources + 1, slot_width, slot_width), jnp.float32),
            pltpu.VMEM((tile_total, 8, slot_width), jnp.float32),
        ],
        compiler_params=pltpu.CompilerParams(vmem_limit_bytes=40 * 1024 * 1024),
        cost_estimate=pl.CostEstimate(
            flops=20 * 9 * tile_total * slot_width * slot_width,
            bytes_accessed=180 * 2**20,
            transcendentals=9 * tile_total * slot_width * slot_width,
        ),
        name="density",
    )(pair_entries, pair_groups, send_index, features, own_form, norm)

    recv_density = lax.all_to_all(
        send_density.reshape(device_total, capacity, slot_width),
        ("gx", "gy"),
        split_axis=0,
        concat_axis=0,
        tiled=True,
    ).reshape(send_rows, slot_width)

    recv_note = recv_state[:, 4, :3]
    recv_slot = recv_note[:, 1].astype(jnp.int32) - 1
    hit = recv_slot[None, :] == tile_order[:, None]
    recv_order = jnp.arange(send_rows, dtype=jnp.int32)
    from_row = jnp.sum(jnp.where(hit, recv_order[None, :], 0), axis=1)
    total_work = jnp.sum(recv_note.reshape(device_total, capacity, 3)[:, 0, 2])
    moved_work = jnp.sum(jnp.where(hit, recv_note[:, 0][None, :], 0.0), axis=1)
    moved_share = moved_work * float(tile_total * device_total) / total_work

    moved_state = pl.pallas_call(
        functools.partial(place_kernel, tile_total),
        out_shape=jax.ShapeDtypeStruct((tile_total, 5, slot_width), jnp.float32),
        in_specs=[SMEM, VMEM, VMEM],
        out_specs=VMEM,
        name="place",
    )(from_row, recv_state, recv_density)
    return (
        moved_state.reshape(rows_local, cols_local, 5, slot_width),
        moved_share.reshape(rows_local, cols_local),
    )


def solution(mesh):
    in_specs = (
        P("gx", "gy", None, None),
        P("gx", "gy", None),
        P("gx", "gy", None),
        P("gx", "gy"),
        P("gx", "gy", None),
        P("gx", "gy"),
    )
    out_specs = (P("gx", "gy", None, None), P("gx", "gy"))
    return jax.shard_map(body, mesh=mesh, in_specs=in_specs, out_specs=out_specs, check_vma=False)
```

time: 325 us -> 159 us (0.49)
  other arithmetic: 168 us -> 10.8 us
  Pallas kernels: 0 us -> 95.2 us
  blocking collectives: 40.5 us -> 0 us
  loops' own time: 23.3 us -> 0 us
  local copies, waits for them, and re-layouts: 47.3 us -> 26.6 us
  waiting for transfers between devices: 18.3 us -> 5.24 us
  starting transfers between devices: 23.8 us -> 18.9 us
    reduce_sum x17 -> x5, other arithmetic: 135 us -> 2.46 us  [the longest x1 0.74 us: body(): total_work = jnp.sum(recv_note.reshape(device_total, capacity, 3)[:, 0, 2])]
    pallas_call x0 -> x3, Pallas kernels: none -> 95.2 us  [the longest x1 86.6 us: body(): pl.pallas_call(functools.partial(density_kernel, tile_total, sources), ou...]
    psum x1 -> x0, blocking collectives: 40.5 us -> none  [body(): total_work = lax.psum(jnp.sum(pair_work), ('gx', 'gy'))]
    another operation x1 -> x0, loops' own time: 23.3 us -> none  [body(): density = lax.map(row_density, jnp.arange(rows_local, dtype=jnp.int32))]
    all_to_all x1, waiting for transfers between devices: 15.5 us -> 0.01 us  [body(): lax.all_to_all(send_state.reshape(device_total, capacity, 5, slot_width),...]
    concatenate x1 -> x8, local copies, waits for them, and re-layouts: 0.21 us -> 13.5 us  [the longest x4 10.3 us: body(): jnp.concatenate([-2.0 * inv_sq * own_x, -2.0 * inv_sq * own_y, -2.0 * inv...]
    add x32 -> x1, other arithmetic: 13.2 us -> 0.01 us  [body(): send_index = target * capacity + rank_slot]
    dynamic_update_slice x8 -> x0, other arithmetic: 11.1 us -> none  [body(): density = lax.map(row_density, jnp.arange(rows_local, dtype=jnp.int32))]
  transfers between devices with their start and end apart: 7 -> 6, of which waited for: 3 -> 2; matrix products, arithmetic and copies ran while one was open for 63% -> 14% of each run, Pallas kernels for 0% -> 59%
where the time goes in v1:
time: 159 us; the launch traced here: 158 us
  Pallas kernels  95.2 us (60%)
  local copies, waits for them, and re-layouts  26.6 us (17%)
  starting transfers between devices  18.9 us (12%)
  other arithmetic  10.8 us (7%)
  waiting for transfers between devices  5.24 us (3%)
    pallas_call x1, Pallas kernels, body(): pl.pallas_call(functools.partial(density_kernel, tile_total, sources), ou...  86.6 us
    concatenate x4, local copies, waits for them, and re-layouts, body(): jnp.concatenate([-2.0 * inv_sq * own_x, -2.0 * inv_sq * own_y, -2.0 * inv...  10.3 us
    all_to_all x1, starting transfers between devices, body(): lax.all_to_all(send_state.reshape(device_total, capacity, 5, slot_width),...  6.28 us
    pallas_call x1, Pallas kernels, body(): pl.pallas_call(functools.partial(list_kernel, rows_local, cols_local), ou...  6.25 us
    ppermute x2, starting transfers between devices, extended(): lax.ppermute(lax.slice_in_dim(block, 0, width, axis=dim), axis, backward)  5.07 us
    all_to_all x1, starting transfers between devices, body(): lax.all_to_all(send_density.reshape(device_total, capacity, slot_width),...  4.77 us
    all_to_all x1, waiting for transfers between devices, body(): lax.all_to_all(send_density.reshape(device_total, capacity, slot_width),...  4.57 us
    scatter x1, local copies, waits for them, and re-layouts, body(): jnp.zeros((send_rows, 5, slot_width), jnp.float32).at[send_index]  4.36 us
  transfers between devices with their start and end apart: 6, of which 2 were waited for; matrix products, arithmetic and copies ran while one was open for 14% of the time, Pallas kernels for 59%

profile of v1, /device:TPU:0, one launch (start us, length us, event | category | flops | bytes accessed | tf_op | source)
XLA Modules:
  0.0 157.7 jit_solution(18247263451750411429)
XLA Ops:
  0.6 1.0 fusion.3
  1.6 0.8 pad_maximum_fusion.3
  2.9 2.0 %collective-permute-start.1 = (f32[1,16,4,128]{3,1,2,0:T(8,128)S(1)}, f32[1,16,4,128]{3,1,2,0:T(8,128)S(1)}, u32[]{:S(2)}, u32[]{:S(2)}) collective-permute-start(f32[1,16,4,128]{3,1,2,0:T(8,128)S(1)} %get-tuple-element.29), channel_id=1, source_target_pairs={{8,0},{16,8},{24,16},{0,24},{9,1},{17,9},{25,17},{1,25},{10,2},{18... | collective-permute-start | bytes 98312 | tf_op jit(solution)/shard_map/ppermute | solution.py:24
  5.9 0.8 copy_convert_fusion
  6.8 1.0 pad_maximum_fusion.7
  7.8 2.3 %collective-permute-start.2 = (f32[10,1,4,128]{3,1,2,0:T(1,128)S(1)}, f32[10,1,4,128]{3,1,2,0:T(1,128)S(1)}, u32[]{:S(2)}, u32[]{:S(2)}) collective-permute-start(f32[10,1,4,128]{3,1,2,0:T(1,128)S(1)} %get-tuple-element.26), channel_id=1, source_target_pairs={{0,1},{1,2},{2,3},{3,4},{4,5},{5,6},{6,7},{7,0},{8,9},{9,10},{10,1... | collective-permute-start | bytes 61448 | tf_op jit(solution)/shard_map/ppermute | solution.py:21
  10.1 3.1 %collective-permute-start.3 = (f32[10,1,4,128]{3,1,2,0:T(1,128)S(1)}, f32[10,1,4,128]{3,1,2,0:T(1,128)S(1)}, u32[]{:S(2)}, u32[]{:S(2)}) collective-permute-start(f32[10,1,4,128]{3,1,2,0:T(1,128)S(1)} %get-tuple-element.27), channel_id=1, source_target_pairs={{1,0},{2,1},{3,2},{4,3},{5,4},{6,5},{7,6},{0,7},{9,8},{10,9},{11,1... | collective-permute-start | bytes 61448 | tf_op jit(solution)/shard_map/ppermute | solution.py:24
  13.2 0.9 copy.41
  14.9 1.0 pad_maximum_fusion
  17.2 4.4 %scatter_fusion = f32[256,5,128]{2,1,0:T(8,128)S(1)} fusion(f32[256,5,128]{2,1,0:T(8,128)S(1)} %broadcast_in_dim.110, s32[128]{0:T(128)S(1)} %fusion.25, f32[128,5,128]{2,1,0:T(8,128)S(1)} %copy.42), kind=kCustom, calls=%fused_computation | custom fusion | bytes 983552 | tf_op jit(solution)/shard_map/scatter | solution.py:201
  22.4 1.0 copy.43
  23.3 6.3 %all-to-all-start = ((f32[32,8,5,128]{3,1,2,0:T(8,128)}), f32[32,8,5,128]{3,1,2,0:T(8,128)}, u32[]{:S(2)}, u32[]{:S(2)}) async-start(f32[32,8,5,128]{3,1,2,0:T(8,128)} %copy.43), calls=%async_computation | async-start | bytes 1310720 | tf_op jit(solution)/shard_map/all_to_all | solution.py:204
  30.5 1.1 add_multiply_fusion
  32.3 0.7 concatenate.44
  33.2 8.8 %concatenate.47.own_ref = f32[128,32,128]{2,1,0:T(8,128)S(1)} concatenate(f32[128,1,128]{2,1,0:T(1,128)} %get-tuple-element.25, f32[128,1,128]{2,1,0:T(1,128)} %get-tuple-element.23, f32[128,1,128]{2,1,0:T(1,128)} %get-tuple-element.24, f32[128,1,128]{2,1,0:T(1,128)S(1)} %bitcast.78, f32[128,1,128]{2,1,0:T(1,128)} %get-tuple-element.22, f32[128,3,128]{2,1,0:T(4,128)S(1)} %broadcast.243, ...), dimensions={1} | concatenate | bytes 4194304 | tf_op jit(solution)/shard_map/concatenate | solution.py:164
  42.0 6.2 %pair_entries.1 = (s32[1160]{0:T(1024)}, s32[1]{0:T(128)}) custom-call(s32[1024]{0:T(1024)} %reshape.271.pair_ref), custom_call_target="tpu_custom_call" | custom-call | flops 4000000 | bytes 8192 | tf_op jit(solution)/shard_map/pair_entries/pallas_call | solution.py:146
  50.2 2.2 %concatenate.43.feat_ref = f32[180,8,128]{2,1,0:T(8,128)S(1)} concatenate(f32[180,3,128]{2,1,0:T(4,128)S(1)} %get-tuple-element.21, f32[180,1,128]{2,1,0:T(1,128)} %broadcast_in_dim.119, f32[180,1,128]{2,1,0:T(1,128)S(1)} %broadcast_in_dim.120, f32[180,1,128]{2,1,0:T(1,128)S(1)} %slice.140, f32[180,2,128]{2,1,0:T(2,128)} %concatenate.42), dimensions={1} | concatenate | bytes 1474560 | tf_op jit(solution)/shard_map/concatenate | solution.py:217
  52.4 86.6 %density.1 = f32[256,128]{1,0:T(8,128)} custom-call(s32[1160]{0:T(1024)S(1)} %copy-done, s32[1]{0:T(128)} %get-tuple-element.5.count_ref, s32[128]{0:T(128)S(1)} %multiply_add_fusion.send_ref, f32[180,8,128]{2,1,0:T(8,128)S(1)} %concatenate.43.feat_ref, f32[128,32,128]{2,1,0:T(8,128)S(1)} %concatenate.47.own_ref, f32[128,128]{1,0:T(8,128)S(1)} %bitcast.63), custom_call_target="tpu_custom_call" | custom-call | flops 377487360 | bytes 188743680 | tf_op jit(solution)/shard_map/density/pallas_call | solution.py:220
  139.1 4.8 %all-to-all-start.1 = ((f32[32,8,128]{2,1,0:T(8,128)}), f32[32,8,128]{2,1,0:T(8,128)S(1)}, u32[]{:S(2)}, u32[]{:S(2)}) async-start(f32[32,8,128]{2,1,0:T(8,128)} %bitcast.21), calls=%async_computation.1 | async-start | bytes 262144 | tf_op jit(solution)/shard_map/all_to_all | solution.py:239
  143.8 1.3 copy.44
  146.3 0.7 slice_reduce_fusion.1
  147.1 4.6 %all-to-all-done.1 = f32[32,8,128]{2,1,0:T(8,128)S(1)} async-done(((f32[32,8,128]{2,1,0:T(8,128)}), f32[32,8,128]{2,1,0:T(8,128)S(1)}, u32[]{:S(2)}, u32[]{:S(2)}) %all-to-all-start.1) | async-done | bytes 131104 | tf_op jit(solution)/shard_map/all_to_all | solution.py:239
  152.3 2.3 %place.1 = f32[128,5,128]{2,1,0:T(8,128)} custom-call(s32[128]{0:T(128)} %select_reduce_fusion.1.from_ref, f32[256,5,128]{2,1,0:T(8,128)} %bitcast.65, f32[256,128]{1,0:T(8,128)} %bitcast.82), custom_call_target="tpu_custom_call" | custom-call | tf_op jit(solution)/shard_map/place/pallas_call | solution.py:256
  154.6 1.8 %copy.48 = f32[8,16,5,128]{3,1,2,0:T(8,128)} copy(f32[8,16,5,128]{3,2,1,0:T(8,128)} %bitcast.67) | data formatting | bytes 655360
  (57 shorter events, 11.1 us)
Async XLA Ops:
  0.6 15.4 %copy-start.5 = (s32[8,16]{1,0:T(8,128)S(1)}, s32[8,16]{1,0:T(8,128)}, u32[]{:S(2)}) copy-start(s32[8,16]{1,0:T(8,128)} %param.9) | copy-start | bytes 1540
  2.4 4.4 %collective-permute-start = (f32[1,16,4,128]{3,1,2,0:T(8,128)S(1)}, f32[1,16,4,128]{3,1,2,0:T(8,128)S(1)}, u32[]{:S(2)}, u32[]{:S(2)}) collective-permute-start(f32[1,16,4,128]{3,1,2,0:T(8,128)S(1)} %get-tuple-element.28), channel_id=1, source_target_pairs={{0,8},{8,16},{16,24},{24,0},{1,9},{9,17},{17,25},{25,1},{2,10},{10... | collective-permute-start | bytes 98312 | tf_op jit(solution)/shard_map/ppermute | solution.py:21
  2.9 3.9 %collective-permute-start.1 = (f32[1,16,4,128]{3,1,2,0:T(8,128)S(1)}, f32[1,16,4,128]{3,1,2,0:T(8,128)S(1)}, u32[]{:S(2)}, u32[]{:S(2)}) collective-permute-start(f32[1,16,4,128]{3,1,2,0:T(8,128)S(1)} %get-tuple-element.29), channel_id=1, source_target_pairs={{8,0},{16,8},{24,16},{0,24},{9,1},{17,9},{25,17},{1,25},{10,2},{18... | collective-permute-start | bytes 98312 | tf_op jit(solution)/shard_map/ppermute | solution.py:24
  7.8 7.1 %collective-permute-start.2 = (f32[10,1,4,128]{3,1,2,0:T(1,128)S(1)}, f32[10,1,4,128]{3,1,2,0:T(1,128)S(1)}, u32[]{:S(2)}, u32[]{:S(2)}) collective-permute-start(f32[10,1,4,128]{3,1,2,0:T(1,128)S(1)} %get-tuple-element.26), channel_id=1, source_target_pairs={{0,1},{1,2},{2,3},{3,4},{4,5},{5,6},{6,7},{7,0},{8,9},{9,10},{10,1... | collective-permute-start | bytes 61448 | tf_op jit(solution)/shard_map/ppermute | solution.py:21
  10.1 4.8 %collective-permute-start.3 = (f32[10,1,4,128]{3,1,2,0:T(1,128)S(1)}, f32[10,1,4,128]{3,1,2,0:T(1,128)S(1)}, u32[]{:S(2)}, u32[]{:S(2)}) collective-permute-start(f32[10,1,4,128]{3,1,2,0:T(1,128)S(1)} %get-tuple-element.27), channel_id=1, source_target_pairs={{1,0},{2,1},{3,2},{4,3},{5,4},{6,5},{7,6},{0,7},{9,8},{10,9},{11,1... | collective-permute-start | bytes 61448 | tf_op jit(solution)/shard_map/ppermute | solution.py:24
  21.6 8.0 %copy-start.4 = (s32[8,16,8]{1,2,0:T(8,128)S(1)}, s32[8,16,8]{1,2,0:T(8,128)}, u32[]{:S(2)}) copy-start(s32[8,16,8]{1,2,0:T(8,128)} %param.10) | copy-start | bytes 12292
  22.3 8.1 %copy-start.1 = (f32[8,16,3,128]{3,1,2,0:T(8,128)S(1)}, f32[8,16,3,128]{3,1,2,0:T(8,128)}, u32[]{:S(2)}) copy-start(f32[8,16,3,128]{3,1,2,0:T(8,128)} %param.6) | copy-start | bytes 589828
  23.3 115.7 %all-to-all-start = ((f32[32,8,5,128]{3,1,2,0:T(8,128)}), f32[32,8,5,128]{3,1,2,0:T(8,128)}, u32[]{:S(2)}, u32[]{:S(2)}) async-start(f32[32,8,5,128]{3,1,2,0:T(8,128)} %copy.43), calls=%async_computation | async-start | bytes 1310720 | tf_op jit(solution)/shard_map/all_to_all | solution.py:204
  48.2 4.2 %copy-start = (s32[1160]{0:T(1024)S(1)}, s32[1160]{0:T(1024)}, u32[]{:S(2)}) copy-start(s32[1160]{0:T(1024)} %get-tuple-element.4.list_ref) | copy-start | bytes 13924
  139.1 12.6 %all-to-all-start.1 = ((f32[32,8,128]{2,1,0:T(8,128)}), f32[32,8,128]{2,1,0:T(8,128)S(1)}, u32[]{:S(2)}, u32[]{:S(2)}) async-start(f32[32,8,128]{2,1,0:T(8,128)} %bitcast.21), calls=%async_computation.1 | async-start | bytes 262144 | tf_op jit(solution)/shard_map/all_to_all | solution.py:239
  145.1 6.5 %copy-start.2 = (f32[32,8,5,128]{3,2,1,0:T(8,128)}, f32[32,8,5,128]{3,2,1,0:T(8,128)S(1)}, u32[]{:S(2)}) copy-start(f32[32,8,5,128]{3,2,1,0:T(8,128)S(1)} %copy.44) | copy-start | bytes 1966084
  151.6 0.7 copy-start.3

commit v2 on v1

v2 whole, which is shorter than its diff:
```python
import functools
import math

import jax
import jax.numpy as jnp
from jax import lax
from jax.experimental import pallas as pl
from jax.experimental.pallas import tpu as pltpu
from jax.sharding import PartitionSpec as P

OFFSETS = tuple((a, b) for a in (-1, 0, 1) for b in (-1, 0, 1) if (a, b) != (0, 0))
UNROLL = 4


def extended(block, sides, width):
    for axis, dim in sides:
        count = lax.axis_size(axis)
        forward = [(i, i + 1) for i in range(count - 1)]
        forward.append((count - 1, 0))
        backward = [(target, source) for source, target in forward]
        low = lax.ppermute(
            lax.slice_in_dim(block, block.shape[dim] - width, None, axis=dim), axis, forward
        )
        high = lax.ppermute(lax.slice_in_dim(block, 0, width, axis=dim), axis, backward)
        block = jnp.concatenate([low, block, high], axis=dim)
    return block


def split3(value):
    high = value.astype(jnp.bfloat16).astype(jnp.float32)
    rest = value - high
    mid = rest.astype(jnp.bfloat16).astype(jnp.float32)
    return high, mid, rest - mid


def density_kernel(
    rows, cols, pair_ref, send_ref, halo_ref, smooth_ref,
    out_ref, lhs_ref, mass_ref, own_ref, sq_ref, acc_ref, list_ref
):
    tiles = rows * cols
    width = smooth_ref.shape[1]
    wide = cols + 2
    sources = (rows + 2) * wide
    row = lax.broadcasted_iota(jnp.int32, (8, width), 0)

    def spread(ref, tile, index):
        return jnp.broadcast_to(ref[tile, index : index + 1, :], (8, width))

    def centre(t):
        tx = t // cols
        return (tx + 1) * wide + (t - tx * cols) + 1

    def point(tile):
        x = spread(halo_ref, tile, 0) - 0.5
        y = spread(halo_ref, tile, 1) - 0.5
        z = spread(halo_ref, tile, 2) - 0.5
        return x, y, z, x * x + y * y + z * z

    def prep(s, ptr):
        x, y, z, norm_sq = point(s)
        root = spread(halo_ref, s, 3)
        feat = jnp.where(row == 0, x, jnp.where(row == 1, y, jnp.where(row == 2, z, 0.0)))
        feat = jnp.where(row == 3, norm_sq, jnp.where(row == 4, 1.0, feat)) * (root * root)
        high, mid, low = split3(feat)
        turned = jnp.concatenate([high, high, mid, mid, high, low, root], axis=0).T
        lhs_ref[s] = turned[:, :48].astype(jnp.bfloat16)
        mass = jnp.broadcast_to(turned[:, 48:49], (width, width))
        mass_ref[s, 0] = mass
        mass_ref[s, 1] = mass + mass

        t = jnp.minimum(s, tiles - 1)
        base = centre(t)
        x, y, z, norm_sq = point(base)
        h = jnp.broadcast_to(smooth_ref[pl.ds(t, 1), :], (8, width))
        inv = 1.0 / (h * h)
        plain = jnp.where(row == 0, x, jnp.where(row == 1, y, z)) * -2.0
        plain = jnp.where(row < 3, plain, jnp.where(row == 3, 1.0, norm_sq))
        own_ref[t, 0] = jnp.where(row < 5, plain * inv, 0.0)
        own_ref[t, 1] = jnp.where(row == 0, 2.0, jnp.where(row == 4, -2.0 * x, 0.0)) * inv
        own_ref[t, 2] = jnp.where(row == 1, 2.0, jnp.where(row == 4, -2.0 * y, 0.0)) * inv
        own_ref[t, 3] = jnp.where(row == 4, inv, 0.0)
        live = jnp.where(s < tiles, 1, 0)
        list_ref[ptr] = (base << 16) | (t << 4) | 5
        ptr = ptr + live
        for k, (a, b) in enumerate(OFFSETS):
            code = (a + 1) * 4 + (b + 1)
            list_ref[ptr] = ((base + a * wide + b) << 16) | (t << 4) | code
            ptr = ptr + jnp.where(pair_ref[t * 8 + k] != 0, live, 0)
        return ptr

    total = lax.fori_loop(0, sources, prep, jnp.int32(0))
    for u in range(3 * UNROLL):
        list_ref[total + u] = (sources << 16) | 5
    lhs_ref[sources] = jnp.zeros((width, 48), jnp.bfloat16)
    mass_ref[sources] = jnp.zeros((2, width, width), jnp.float32)
    acc_ref[...] = jnp.zeros_like(acc_ref)
    out_ref[...] = jnp.zeros_like(out_ref)

    def products(first, slot):
        for u in range(UNROLL):
            entry = list_ref[first + u]
            t = (entry >> 4) & 4095
            off_x = (((entry >> 2) & 3) - 1).astype(jnp.float32)
            off_y = ((entry & 3) - 1).astype(jnp.float32)
            off_sq = off_x * off_x + off_y * off_y
            form = own_ref[t, 0] + off_x * own_ref[t, 1] + off_y * own_ref[t, 2] + off_sq * own_ref[t, 3]
            high, mid, low = split3(form)
            rhs = jnp.concatenate([high, mid, high, mid, low, high], axis=0).astype(jnp.bfloat16)
            sq_ref[slot, u] = jnp.dot(
                lhs_ref[entry >> 16], rhs, preferred_element_type=jnp.float32
            )

    def sums(first, slot):
        for u in range(UNROLL):
            entry = list_ref[first + u]
            source = entry >> 16
            t = (entry >> 4) & 4095
            outer_sum = jnp.zeros((8, width), jnp.float32)
            inner_sum = jnp.zeros((8, width), jnp.float32)
            for g in range(width // 8):
                at = pl.ds(8 * g, 8)
                sq = jnp.maximum(sq_ref[slot, u, at, :], 1e-20)
                ratio = sq * lax.rsqrt(sq)
                outer = jnp.maximum(mass_ref[source, 1, at, :] - ratio, 0.0)
                inner = jnp.maximum(mass_ref[source, 0, at, :] - ratio, 0.0)
                outer_sum = outer_sum + outer * outer * outer
                inner_sum = inner_sum + inner * inner * inner
            acc_ref[t] += outer_sum - 4.0 * inner_sum

    products(0, 0)

    def step(i, carry):
        first = i * (2 * UNROLL)
        products(first + UNROLL, 1)
        sums(first, 0)
        products(first + 2 * UNROLL, 0)
        sums(first + UNROLL, 1)
        return carry

    lax.fori_loop(0, (total + 2 * UNROLL - 1) // (2 * UNROLL), step, 0)

    def finish(t, carry):
        summed = jnp.sum(acc_ref[t], axis=0, keepdims=True)
        h = smooth_ref[pl.ds(t, 1), :]
        norm = 0.25 / (math.pi * h * h * h)
        alive = halo_ref[centre(t), 3:4, :] > 0.0
        out_ref[pl.ds(send_ref[t], 1), :] = jnp.where(alive, summed * norm, 0.0)
        return carry

    lax.fori_loop(0, tiles, finish, 0, unroll=4)


def place_kernel(tiles, from_ref, state_ref, dens_ref, out_ref):
    def put(s, carry):
        row = from_ref[s]
        out_ref[s, 0:4, :] = state_ref[row, 0:4, :]
        out_ref[s, 4:5, :] = dens_ref[pl.ds(row, 1), :]
        return carry

    lax.fori_loop(0, tiles, put, 0, unroll=8)


SMEM = pl.BlockSpec(memory_space=pltpu.SMEM)
VMEM = pl.BlockSpec(memory_space=pltpu.VMEM)


def body(positions, masses, smoothing, counts, pair_list, dest):
    rows_local, cols_local = counts.shape
    slot_width = masses.shape[2]
    grid_x = lax.axis_size("gx")
    grid_y = lax.axis_size("gy")
    device_total = grid_x * grid_y
    tile_total = rows_local * cols_local
    capacity = max(2, 2 * tile_total // device_total)
    send_rows = device_total * capacity
    slot_ids = jnp.arange(slot_width, dtype=jnp.int32)
    valid_slot = slot_ids[None, None, :] < counts[:, :, None]
    masked = jnp.where(valid_slot, masses, jnp.zeros_like(masses))
    packed = jnp.concatenate([positions, masked[:, :, None, :]], axis=2)
    root = jnp.where(valid_slot, jnp.cbrt(masses), jnp.zeros_like(masses))
    rooted = jnp.concatenate([positions, root[:, :, None, :]], axis=2)
    padded = extended(rooted, (("gx", 0), ("gy", 1)), 1)
    weights = pair_list.astype(jnp.float32)

    row_span = cols_local * grid_y
    slot_x = dest // row_span
    slot_y = dest % row_span
    target = (slot_x // rows_local * grid_y + slot_y // cols_local).reshape(-1)
    slot_local = (slot_x % rows_local * cols_local + slot_y % cols_local).reshape(-1)
    tile_order = jnp.arange(tile_total, dtype=jnp.int32)
    same_target = target[:, None] == target[None, :]
    earlier = tile_order[None, :] < tile_order[:, None]
    rank_slot = jnp.sum(jnp.logical_and(same_target, earlier).astype(jnp.int32), axis=1)
    send_index = target * capacity + rank_slot

    tile_count = counts.astype(jnp.float32)
    padded_count = jnp.sum((padded[:, :, 3, :] > 0.0).astype(jnp.float32), axis=-1)
    neighbour_sum = jnp.zeros((rows_local, cols_local), jnp.float32)
    for k, (a, b) in enumerate(OFFSETS):
        beside = padded_count[1 + a : 1 + a + rows_local, 1 + b : 1 + b + cols_local]
        neighbour_sum = neighbour_sum + weights[:, :, k] * beside
    pair_work = tile_count * (tile_count + neighbour_sum)
    local_work = jnp.sum(pair_work)

    lane = slot_ids[None, :]
    note = jnp.where(lane == 0, pair_work.reshape(-1, 1), 0.0)
    note = jnp.where(lane == 1, (slot_local + 1).astype(jnp.float32)[:, None], note)
    tile_state = jnp.concatenate(
        [packed.reshape(tile_total, 4, slot_width), note[:, None, :]], axis=1
    )
    send_state = jnp.zeros((send_rows, 5, slot_width), jnp.float32).at[send_index].set(tile_state)
    mark = jnp.logical_and(jnp.arange(5)[:, None] == 4, lane == 2)
    send_state = jnp.where(mark[None], local_work, send_state)
    recv_state = lax.all_to_all(
        send_state.reshape(device_total, capacity, 5, slot_width),
        ("gx", "gy"),
        split_axis=0,
        concat_axis=0,
        tiled=True,
    ).reshape(send_rows, 5, slot_width)

    sources = (rows_local + 2) * (cols_local + 2)
    send_density = pl.pallas_call(
        functools.partial(density_kernel, rows_local, cols_local),
        out_shape=jax.ShapeDtypeStruct((send_rows, slot_width), jnp.float32),
        in_specs=[SMEM, SMEM, VMEM, VMEM],
        out_specs=VMEM,
        scratch_shapes=[
            pltpu.VMEM((sources + 1, slot_width, 48), jnp.bfloat16),
            pltpu.VMEM((sources + 1, 2, slot_width, slot_width), jnp.float32),
            pltpu.VMEM((tile_total, 4, 8, slot_width), jnp.float32),
            pltpu.VMEM((2, UNROLL, slot_width, slot_width), jnp.float32),
            pltpu.VMEM((tile_total, 8, slot_width), jnp.float32),
            pltpu.SMEM((9 * tile_total + 4 * UNROLL,), jnp.int32),
        ],
        compiler_params=pltpu.CompilerParams(vmem_limit_bytes=52 * 1024 * 1024),
        cost_estimate=pl.CostEstimate(
            flops=20 * 9 * tile_total * slot_width * slot_width,
            bytes_accessed=180 * 2**20,
            transcendentals=9 * tile_total * slot_width * slot_width,
        ),
        name="density",
    )(
        pair_list.reshape(-1),
        send_index,
        padded.reshape(sources, 4, slot_width),
        smoothing.reshape(tile_total, slot_width),
    )

    recv_density = lax.all_to_all(
        send_density.reshape(device_total, capacity, slot_width),
        ("gx", "gy"),
        split_axis=0,
        concat_axis=0,
        tiled=True,
    ).reshape(send_rows, slot_width)

    recv_note = recv_state[:, 4, :3]
    recv_slot = recv_note[:, 1].astype(jnp.int32) - 1
    hit = recv_slot[None, :] == tile_order[:, None]
    recv_order = jnp.arange(send_rows, dtype=jnp.int32)
    from_row = jnp.sum(jnp.where(hit, recv_order[None, :], 0), axis=1)
    total_work = jnp.sum(recv_note.reshape(device_total, capacity, 3)[:, 0, 2])
    moved_work = jnp.sum(jnp.where(hit, recv_note[:, 0][None, :], 0.0), axis=1)
    moved_share = moved_work * float(tile_total * device_total) / total_work

    moved_state = pl.pallas_call(
        functools.partial(place_kernel, tile_total),
        out_shape=jax.ShapeDtypeStruct((tile_total, 5, slot_width), jnp.float32),
        in_specs=[SMEM, VMEM, VMEM],
        out_specs=VMEM,
        name="place",
    )(from_row, recv_state, recv_density)
    return (
        moved_state.reshape(rows_local, cols_local, 5, slot_width),
        moved_share.reshape(rows_local, cols_local),
    )


def solution(mesh):
    in_specs = (
        P("gx", "gy", None, None),
        P("gx", "gy", None),
        P("gx", "gy", None),
        P("gx", "gy"),
        P("gx", "gy", None),
        P("gx", "gy"),
    )
    out_specs = (P("gx", "gy", None, None), P("gx", "gy"))
    return jax.shard_map(body, mesh=mesh, in_specs=in_specs, out_specs=out_specs, check_vma=False)
```

time: 159 us -> 130 us (0.82); the launches traced: 158 us -> 131 us
  local copies, waits for them, and re-layouts: 26.6 us -> 11.1 us
  Pallas kernels: 95.2 us -> 84 us
  other arithmetic: 10.8 us -> 5.29 us
  waiting for transfers between devices: 5.24 us -> 8.46 us
  starting transfers between devices: 18.9 us -> 20.9 us
    concatenate x6 -> x0, local copies, waits for them, and re-layouts: 13.2 us -> none  [the longest x4 10.3 us: body(): jnp.concatenate([-2.0 * inv_sq * own_x, -2.0 * inv_sq * own_y, -2.0 * inv...]
    pallas_call x2 -> x1, Pallas kernels: 92.9 us -> 81.7 us  [body(): pl.pallas_call(functools.partial(density_kernel, rows_local, cols_local),...]
    ppermute x2, waiting for transfers between devices: 0.67 us -> 2.63 us  [extended(): lax.ppermute(lax.slice_in_dim(block, block.shape[dim] - width, None, axis...]
    all_to_all x1, starting transfers between devices: 4.77 us -> 6.57 us  [body(): lax.all_to_all(send_density.reshape(device_total, capacity, slot_width),...]
    slice x2, other arithmetic: 1.75 us -> 0.04 us  [extended(): lax.slice_in_dim(block, block.shape[dim] - width, None, axis=dim)]
    unnamed x15 -> x17, local copies, waits for them, and re-layouts: 3.52 us -> 3.88 us
  transfers between devices with their start and end apart: 6 -> 6, of which waited for: 2 -> 4; matrix products, arithmetic and copies ran while one was open for 14% -> 2% of each run, Pallas kernels for 59% -> 63%
where the time goes in v2:
time: 130 us; the launch traced here: 131 us
  Pallas kernels  84 us (65%)
  starting transfers between devices  20.9 us (16%)
  local copies, waits for them, and re-layouts  11.1 us (9%)
  waiting for transfers between devices  8.46 us (7%)
  other arithmetic  5.29 us (4%)
    pallas_call x1, Pallas kernels, body(): pl.pallas_call(functools.partial(density_kernel, rows_local, cols_local),...  81.7 us
    all_to_all x1, starting transfers between devices, body(): lax.all_to_all(send_density.reshape(device_total, capacity, slot_width),...  6.57 us
    all_to_all x1, starting transfers between devices, body(): lax.all_to_all(send_state.reshape(device_total, capacity, 5, slot_width),...  6.44 us
    all_to_all x1, waiting for transfers between devices, body(): lax.all_to_all(send_density.reshape(device_total, capacity, slot_width),...  5.65 us
    ppermute x2, starting transfers between devices, extended(): lax.ppermute(lax.slice_in_dim(block, 0, width, axis=dim), axis, backward)  5.08 us
    scatter x1, local copies, waits for them, and re-layouts, body(): jnp.zeros((send_rows, 5, slot_width), jnp.float32).at[send_index]  4.36 us
    unnamed x17, local copies, waits for them, and re-layouts  3.88 us
    ppermute x2, starting transfers between devices, extended(): lax.ppermute(lax.slice_in_dim(block, block.shape[dim] - width, None, axis...  2.76 us
  transfers between devices with their start and end apart: 6, of which 4 were waited for; matrix products, arithmetic and copies ran while one was open for 2% of the time, Pallas kernels for 63%

profile of v2, /device:TPU:0, one launch (start us, length us, event | category | flops | bytes accessed | tf_op | source)
XLA Modules:
  0.0 130.6 jit_solution(12823676897321620106)
XLA Ops:
  0.6 1.0 fusion.2
  1.7 0.5 collective-permute-start
  2.2 2.0 %collective-permute-start.1 = (f32[1,16,4,128]{3,1,2,0:T(8,128)S(1)}, f32[1,16,4,128]{3,1,2,0:T(8,128)S(1)}, u32[]{:S(2)}, u32[]{:S(2)}) collective-permute-start(f32[1,16,4,128]{3,1,2,0:T(8,128)S(1)} %get-tuple-element.19), channel_id=1, source_target_pairs={{8,0},{16,8},{24,16},{0,24},{9,1},{17,9},{25,17},{1,25},{10,2},{18... | collective-permute-start | bytes 98312 | tf_op jit(solution)/shard_map/ppermute | solution.py:24
  4.7 1.0 collective-permute-done
  5.9 2.2 %collective-permute-start.2 = (f32[10,1,4,128]{3,1,2,0:T(1,128)S(1)}, f32[10,1,4,128]{3,1,2,0:T(1,128)S(1)}, u32[]{:S(2)}, u32[]{:S(2)}) collective-permute-start(f32[10,1,4,128]{3,1,2,0:T(1,128)S(1)} %get-tuple-element.16), channel_id=1, source_target_pairs={{0,1},{1,2},{2,3},{3,4},{4,5},{5,6},{6,7},{7,0},{8,9},{9,10},{10,1... | collective-permute-start | bytes 61448 | tf_op jit(solution)/shard_map/ppermute | solution.py:21
  8.1 3.1 %collective-permute-start.3 = (f32[10,1,4,128]{3,1,2,0:T(1,128)S(1)}, f32[10,1,4,128]{3,1,2,0:T(1,128)S(1)}, u32[]{:S(2)}, u32[]{:S(2)}) collective-permute-start(f32[10,1,4,128]{3,1,2,0:T(1,128)S(1)} %get-tuple-element.17), channel_id=1, source_target_pairs={{1,0},{2,1},{3,2},{4,3},{5,4},{6,5},{7,6},{0,7},{9,8},{10,9},{11,1... | collective-permute-start | bytes 61448 | tf_op jit(solution)/shard_map/ppermute | solution.py:24
  11.3 1.6 %collective-permute-done.2 = f32[10,1,4,128]{3,1,2,0:T(1,128)S(1)} collective-permute-done((f32[10,1,4,128]{3,1,2,0:T(1,128)S(1)}, f32[10,1,4,128]{3,1,2,0:T(1,128)S(1)}, u32[]{:S(2)}, u32[]{:S(2)}) %collective-permute-start.2) | collective-permute-done | bytes 20512 | tf_op jit(solution)/shard_map/ppermute | solution.py:21
  13.2 0.6 copy-done.5
  13.7 0.7 fusion.24
  14.9 4.4 %scatter_fusion = f32[256,5,128]{2,1,0:T(8,128)S(1)} fusion(f32[256,5,128]{2,1,0:T(8,128)S(1)} %broadcast_in_dim.99, s32[128]{0:T(128)S(1)} %fusion.23, f32[128,5,128]{2,1,0:T(8,128)S(1)} %copy.38), kind=kCustom, calls=%fused_computation | custom fusion | bytes 983552 | tf_op jit(solution)/shard_map/scatter | solution.py:211
  19.3 0.7 broadcast_select_fusion
  20.0 1.0 copy.39
  21.0 6.4 %all-to-all-start = ((f32[32,8,5,128]{3,1,2,0:T(8,128)}), f32[32,8,5,128]{3,1,2,0:T(8,128)S(1)}, u32[]{:S(2)}, u32[]{:S(2)}) async-start(f32[32,8,5,128]{3,1,2,0:T(8,128)} %copy.39), calls=%async_computation | async-start | bytes 1310720 | tf_op jit(solution)/shard_map/all_to_all | solution.py:214
  27.7 0.7 copy-done
  28.4 81.7 %density.1 = f32[256,128]{1,0:T(8,128)} custom-call(s32[1024]{0:T(1024)S(1)} %reshape.232.pair_ref, s32[128]{0:T(128)S(1)} %multiply_add_fusion.send_ref, f32[180,4,128]{2,1,0:T(4,128)S(1)} %bitcast.62, f32[128,128]{1,0:T(8,128)S(1)} %bitcast.63), custom_call_target="tpu_custom_call" | custom-call | flops 377487360 | bytes 188743680 | tf_op jit(solution)/shard_map/density/pallas_call | solution.py:223
  110.2 6.6 %all-to-all-start.1 = ((f32[32,8,128]{2,1,0:T(8,128)}), f32[32,8,128]{2,1,0:T(8,128)S(1)}, u32[]{:S(2)}, u32[]{:S(2)}) async-start(f32[32,8,128]{2,1,0:T(8,128)} %bitcast.19), calls=%async_computation.1 | async-start | bytes 262144 | tf_op jit(solution)/shard_map/all_to_all | solution.py:250
  117.4 0.6 select_reduce_fusion.1.from_ref
  118.2 0.7 slice_reduce_fusion.1
  118.9 5.7 %all-to-all-done.1 = f32[32,8,128]{2,1,0:T(8,128)S(1)} async-done(((f32[32,8,128]{2,1,0:T(8,128)}), f32[32,8,128]{2,1,0:T(8,128)S(1)}, u32[]{:S(2)}, u32[]{:S(2)}) %all-to-all-start.1) | async-done | bytes 131104 | tf_op jit(solution)/shard_map/all_to_all | solution.py:250
  124.6 0.7 copy-done.3
  125.2 2.3 %place.1 = f32[128,5,128]{2,1,0:T(8,128)} custom-call(s32[128]{0:T(128)} %select_reduce_fusion.1.from_ref, f32[256,5,128]{2,1,0:T(8,128)} %bitcast.65, f32[256,128]{1,0:T(8,128)} %bitcast.72), custom_call_target="tpu_custom_call" | custom-call | tf_op jit(solution)/shard_map/place/pallas_call | solution.py:267
  127.5 1.8 %copy.43 = f32[8,16,5,128]{3,1,2,0:T(8,128)} copy(f32[8,16,5,128]{3,2,1,0:T(8,128)} %bitcast.67) | data formatting | bytes 655360
  129.3 0.6 multiply_divide_fusion
  130.0 0.7 div.56
  (44 shorter events, 2.5 us)
Async XLA Ops:
  0.6 1.0 copy-start.2
  1.6 2.6 %copy-start.6 = (s32[8,16]{1,0:T(8,128)S(1)}, s32[8,16]{1,0:T(8,128)}, u32[]{:S(2)}) copy-start(s32[8,16]{1,0:T(8,128)} %param.11) | copy-start | bytes 1540
  1.6 2.9 %copy-start.4 = (s32[8,16,8]{1,2,0:T(8,128)S(1)}, s32[8,16,8]{1,2,0:T(8,128)}, u32[]{:S(2)}) copy-start(s32[8,16,8]{1,2,0:T(8,128)} %param.10) | copy-start | bytes 12292
  1.7 4.1 %collective-permute-start = (f32[1,16,4,128]{3,1,2,0:T(8,128)S(1)}, f32[1,16,4,128]{3,1,2,0:T(8,128)S(1)}, u32[]{:S(2)}, u32[]{:S(2)}) collective-permute-start(f32[1,16,4,128]{3,1,2,0:T(8,128)S(1)} %get-tuple-element.18), channel_id=1, source_target_pairs={{0,8},{8,16},{16,24},{24,0},{1,9},{9,17},{17,25},{25,1},{2,10},{10... | collective-permute-start | bytes 98312 | tf_op jit(solution)/shard_map/ppermute | solution.py:21
  2.2 3.7 %collective-permute-start.1 = (f32[1,16,4,128]{3,1,2,0:T(8,128)S(1)}, f32[1,16,4,128]{3,1,2,0:T(8,128)S(1)}, u32[]{:S(2)}, u32[]{:S(2)}) collective-permute-start(f32[1,16,4,128]{3,1,2,0:T(8,128)S(1)} %get-tuple-element.19), channel_id=1, source_target_pairs={{8,0},{16,8},{24,16},{0,24},{9,1},{17,9},{25,17},{1,25},{10,2},{18... | collective-permute-start | bytes 98312 | tf_op jit(solution)/shard_map/ppermute | solution.py:24
  5.9 7.0 %collective-permute-start.2 = (f32[10,1,4,128]{3,1,2,0:T(1,128)S(1)}, f32[10,1,4,128]{3,1,2,0:T(1,128)S(1)}, u32[]{:S(2)}, u32[]{:S(2)}) collective-permute-start(f32[10,1,4,128]{3,1,2,0:T(1,128)S(1)} %get-tuple-element.16), channel_id=1, source_target_pairs={{0,1},{1,2},{2,3},{3,4},{4,5},{5,6},{6,7},{7,0},{8,9},{9,10},{10,1... | collective-permute-start | bytes 61448 | tf_op jit(solution)/shard_map/ppermute | solution.py:21
  8.1 4.8 %collective-permute-start.3 = (f32[10,1,4,128]{3,1,2,0:T(1,128)S(1)}, f32[10,1,4,128]{3,1,2,0:T(1,128)S(1)}, u32[]{:S(2)}, u32[]{:S(2)}) collective-permute-start(f32[10,1,4,128]{3,1,2,0:T(1,128)S(1)} %get-tuple-element.17), channel_id=1, source_target_pairs={{1,0},{2,1},{3,2},{4,3},{5,4},{6,5},{7,6},{0,7},{9,8},{10,9},{11,1... | collective-permute-start | bytes 61448 | tf_op jit(solution)/shard_map/ppermute | solution.py:24
  13.0 0.7 copy-start.5
  21.0 89.2 %all-to-all-start = ((f32[32,8,5,128]{3,1,2,0:T(8,128)}), f32[32,8,5,128]{3,1,2,0:T(8,128)S(1)}, u32[]{:S(2)}, u32[]{:S(2)}) async-start(f32[32,8,5,128]{3,1,2,0:T(8,128)} %copy.39), calls=%async_computation | async-start | bytes 1310720 | tf_op jit(solution)/shard_map/all_to_all | solution.py:214
  27.6 0.8 copy-start
  110.2 14.4 %all-to-all-start.1 = ((f32[32,8,128]{2,1,0:T(8,128)}), f32[32,8,128]{2,1,0:T(8,128)S(1)}, u32[]{:S(2)}, u32[]{:S(2)}) async-start(f32[32,8,128]{2,1,0:T(8,128)} %bitcast.19), calls=%async_computation.1 | async-start | bytes 262144 | tf_op jit(solution)/shard_map/all_to_all | solution.py:250
  117.0 7.6 %copy-start.1 = (f32[32,8,5,128]{3,2,1,0:T(8,128)}, f32[32,8,5,128]{3,2,1,0:T(8,128)S(1)}, u32[]{:S(2)}) copy-start(f32[32,8,5,128]{3,2,1,0:T(8,128)S(1)} %copy.40) | copy-start | bytes 1966084
  124.6 0.7 copy-start.3

commit v3 on v2

--- a/solution.py
+++ b/solution.py
@@ -79,16 +79,15 @@
         own_ref[t, 1] = jnp.where(row == 0, 2.0, jnp.where(row == 4, -2.0 * x, 0.0)) * inv
         own_ref[t, 2] = jnp.where(row == 1, 2.0, jnp.where(row == 4, -2.0 * y, 0.0)) * inv
         own_ref[t, 3] = jnp.where(row == 4, inv, 0.0)
-        live = jnp.where(s < tiles, 1, 0)
-        list_ref[ptr] = (base << 16) | (t << 4) | 5
-        ptr = ptr + live
+        middle = (base << 16) | (t << 4) | 5
+        list_ref[ptr] = middle
+        end = ptr + 1
         for k, (a, b) in enumerate(OFFSETS):
-            code = (a + 1) * 4 + (b + 1)
-            list_ref[ptr] = ((base + a * wide + b) << 16) | (t << 4) | code
-            ptr = ptr + jnp.where(pair_ref[t * 8 + k] != 0, live, 0)
-        return ptr
-
-    total = lax.fori_loop(0, sources, prep, jnp.int32(0))
+            list_ref[end] = middle + ((a * wide + b) * 65536 + a * 4 + b)
+            end = end + pair_ref[t * 8 + k]
+        return jnp.where(s < tiles, end, ptr)
+
+    total = lax.fori_loop(0, sources, prep, jnp.int32(0), unroll=4 if sources % 4 == 0 else 1)
     for u in range(3 * UNROLL):
         list_ref[total + u] = (sources << 16) | 5
     lhs_ref[sources] = jnp.zeros((width, 48), jnp.bfloat16)

time: 130 us -> 110 us (0.85)
  Pallas kernels: 84 us -> 64.4 us
    pallas_call x1, Pallas kernels: 81.7 us -> 62.1 us  [body(): pl.pallas_call(functools.partial(density_kernel, rows_local, cols_local),...]
  transfers between devices with their start and end apart: 6 -> 6, of which waited for: 4 -> 4; matrix products, arithmetic and copies ran while one was open for 2% -> 3% of each run, Pallas kernels for 63% -> 57%
where the time goes in v3:
time: 110 us
  Pallas kernels  64.4 us (59%)
  starting transfers between devices  19.6 us (18%)
  local copies, waits for them, and re-layouts  11.1 us (10%)
  waiting for transfers between devices  8.46 us (8%)
  other arithmetic  5.29 us (5%)
    pallas_call x1, Pallas kernels, body(): pl.pallas_call(functools.partial(density_kernel, rows_local, cols_local),...  62.1 us
    all_to_all x1, starting transfers between devices, body(): lax.all_to_all(send_state.reshape(device_total, capacity, 5, slot_width),...  6.44 us
    all_to_all x1, waiting for transfers between devices, body(): lax.all_to_all(send_density.reshape(device_total, capacity, slot_width),...  5.65 us
    all_to_all x1, starting transfers between devices, body(): lax.all_to_all(send_density.reshape(device_total, capacity, slot_width),...  5.34 us
    ppermute x2, starting transfers between devices, extended(): lax.ppermute(lax.slice_in_dim(block, 0, width, axis=dim), axis, backward)  5.08 us
    scatter x1, local copies, waits for them, and re-layouts, body(): jnp.zeros((send_rows, 5, slot_width), jnp.float32).at[send_index]  4.36 us
    unnamed x17, local copies, waits for them, and re-layouts  3.88 us
    ppermute x2, starting transfers between devices, extended(): lax.ppermute(lax.slice_in_dim(block, block.shape[dim] - width, None, axis...  2.76 us
  transfers between devices with their start and end apart: 6, of which 4 were waited for; matrix products, arithmetic and copies ran while one was open for 3% of the time, Pallas kernels for 57%

profile of v3, /device:TPU:0, one launch (start us, length us, event | category | flops | bytes accessed | tf_op | source)
XLA Modules:
  0.0 109.7 jit_solution(13113347172434602229)
XLA Ops:
  0.6 1.0 fusion.2
  1.7 0.5 collective-permute-start
  2.2 2.0 %collective-permute-start.1 = (f32[1,16,4,128]{3,1,2,0:T(8,128)S(1)}, f32[1,16,4,128]{3,1,2,0:T(8,128)S(1)}, u32[]{:S(2)}, u32[]{:S(2)}) collective-permute-start(f32[1,16,4,128]{3,1,2,0:T(8,128)S(1)} %get-tuple-element.19), channel_id=1, source_target_pairs={{8,0},{16,8},{24,16},{0,24},{9,1},{17,9},{25,17},{1,25},{10,2},{18... | collective-permute-start | bytes 98312 | tf_op jit(solution)/shard_map/ppermute | solution.py:24
  4.7 1.0 collective-permute-done
  5.9 2.2 %collective-permute-start.2 = (f32[10,1,4,128]{3,1,2,0:T(1,128)S(1)}, f32[10,1,4,128]{3,1,2,0:T(1,128)S(1)}, u32[]{:S(2)}, u32[]{:S(2)}) collective-permute-start(f32[10,1,4,128]{3,1,2,0:T(1,128)S(1)} %get-tuple-element.16), channel_id=1, source_target_pairs={{0,1},{1,2},{2,3},{3,4},{4,5},{5,6},{6,7},{7,0},{8,9},{9,10},{10,1... | collective-permute-start | bytes 61448 | tf_op jit(solution)/shard_map/ppermute | solution.py:21
  8.1 3.1 %collective-permute-start.3 = (f32[10,1,4,128]{3,1,2,0:T(1,128)S(1)}, f32[10,1,4,128]{3,1,2,0:T(1,128)S(1)}, u32[]{:S(2)}, u32[]{:S(2)}) collective-permute-start(f32[10,1,4,128]{3,1,2,0:T(1,128)S(1)} %get-tuple-element.17), channel_id=1, source_target_pairs={{1,0},{2,1},{3,2},{4,3},{5,4},{6,5},{7,6},{0,7},{9,8},{10,9},{11,1... | collective-permute-start | bytes 61448 | tf_op jit(solution)/shard_map/ppermute | solution.py:24
  11.3 1.6 %collective-permute-done.2 = f32[10,1,4,128]{3,1,2,0:T(1,128)S(1)} collective-permute-done((f32[10,1,4,128]{3,1,2,0:T(1,128)S(1)}, f32[10,1,4,128]{3,1,2,0:T(1,128)S(1)}, u32[]{:S(2)}, u32[]{:S(2)}) %collective-permute-start.2) | collective-permute-done | bytes 20512 | tf_op jit(solution)/shard_map/ppermute | solution.py:21
  13.2 0.6 copy-done.5
  13.7 0.7 fusion.24
  14.9 4.4 %scatter_fusion = f32[256,5,128]{2,1,0:T(8,128)S(1)} fusion(f32[256,5,128]{2,1,0:T(8,128)S(1)} %broadcast_in_dim.99, s32[128]{0:T(128)S(1)} %fusion.23, f32[128,5,128]{2,1,0:T(8,128)S(1)} %copy.38), kind=kCustom, calls=%fused_computation | custom fusion | bytes 983552 | tf_op jit(solution)/shard_map/scatter | solution.py:210
  19.3 0.7 broadcast_select_fusion
  20.0 1.0 copy.39
  21.0 6.4 %all-to-all-start = ((f32[32,8,5,128]{3,1,2,0:T(8,128)}), f32[32,8,5,128]{3,1,2,0:T(8,128)S(1)}, u32[]{:S(2)}, u32[]{:S(2)}) async-start(f32[32,8,5,128]{3,1,2,0:T(8,128)} %copy.39), calls=%async_computation | async-start | bytes 1310720 | tf_op jit(solution)/shard_map/all_to_all | solution.py:213
  27.7 0.7 copy-done
  28.4 62.1 %density.1 = f32[256,128]{1,0:T(8,128)} custom-call(s32[1024]{0:T(1024)S(1)} %reshape.232.pair_ref, s32[128]{0:T(128)S(1)} %multiply_add_fusion.send_ref, f32[180,4,128]{2,1,0:T(4,128)S(1)} %bitcast.62, f32[128,128]{1,0:T(8,128)S(1)} %bitcast.63), custom_call_target="tpu_custom_call" | custom-call | flops 377487360 | bytes 188743680 | tf_op jit(solution)/shard_map/density/pallas_call | solution.py:222
  90.5 5.3 %all-to-all-start.1 = ((f32[32,8,128]{2,1,0:T(8,128)}), f32[32,8,128]{2,1,0:T(8,128)S(1)}, u32[]{:S(2)}, u32[]{:S(2)}) async-start(f32[32,8,128]{2,1,0:T(8,128)} %bitcast.19), calls=%async_computation.1 | async-start | bytes 262144 | tf_op jit(solution)/shard_map/all_to_all | solution.py:249
  96.5 0.6 select_reduce_fusion.1.from_ref
  97.3 0.7 slice_reduce_fusion.1
  98.0 5.7 %all-to-all-done.1 = f32[32,8,128]{2,1,0:T(8,128)S(1)} async-done(((f32[32,8,128]{2,1,0:T(8,128)}), f32[32,8,128]{2,1,0:T(8,128)S(1)}, u32[]{:S(2)}, u32[]{:S(2)}) %all-to-all-start.1) | async-done | bytes 131104 | tf_op jit(solution)/shard_map/all_to_all | solution.py:249
  103.7 0.7 copy-done.3
  104.3 2.3 %place.1 = f32[128,5,128]{2,1,0:T(8,128)} custom-call(s32[128]{0:T(128)} %select_reduce_fusion.1.from_ref, f32[256,5,128]{2,1,0:T(8,128)} %bitcast.65, f32[256,128]{1,0:T(8,128)} %bitcast.72), custom_call_target="tpu_custom_call" | custom-call | tf_op jit(solution)/shard_map/place/pallas_call | solution.py:266
  106.6 1.8 %copy.43 = f32[8,16,5,128]{3,1,2,0:T(8,128)} copy(f32[8,16,5,128]{3,2,1,0:T(8,128)} %bitcast.67) | data formatting | bytes 655360
  108.5 0.6 multiply_divide_fusion
  109.1 0.7 div.56
  (44 shorter events, 2.5 us)
Async XLA Ops:
  0.6 1.0 copy-start.2
  1.6 2.6 %copy-start.6 = (s32[8,16]{1,0:T(8,128)S(1)}, s32[8,16]{1,0:T(8,128)}, u32[]{:S(2)}) copy-start(s32[8,16]{1,0:T(8,128)} %param.11) | copy-start | bytes 1540
  1.6 2.9 %copy-start.4 = (s32[8,16,8]{1,2,0:T(8,128)S(1)}, s32[8,16,8]{1,2,0:T(8,128)}, u32[]{:S(2)}) copy-start(s32[8,16,8]{1,2,0:T(8,128)} %param.10) | copy-start | bytes 12292
  1.7 4.1 %collective-permute-start = (f32[1,16,4,128]{3,1,2,0:T(8,128)S(1)}, f32[1,16,4,128]{3,1,2,0:T(8,128)S(1)}, u32[]{:S(2)}, u32[]{:S(2)}) collective-permute-start(f32[1,16,4,128]{3,1,2,0:T(8,128)S(1)} %get-tuple-element.18), channel_id=1, source_target_pairs={{0,8},{8,16},{16,24},{24,0},{1,9},{9,17},{17,25},{25,1},{2,10},{10... | collective-permute-start | bytes 98312 | tf_op jit(solution)/shard_map/ppermute | solution.py:21
  2.2 3.7 %collective-permute-start.1 = (f32[1,16,4,128]{3,1,2,0:T(8,128)S(1)}, f32[1,16,4,128]{3,1,2,0:T(8,128)S(1)}, u32[]{:S(2)}, u32[]{:S(2)}) collective-permute-start(f32[1,16,4,128]{3,1,2,0:T(8,128)S(1)} %get-tuple-element.19), channel_id=1, source_target_pairs={{8,0},{16,8},{24,16},{0,24},{9,1},{17,9},{25,17},{1,25},{10,2},{18... | collective-permute-start | bytes 98312 | tf_op jit(solution)/shard_map/ppermute | solution.py:24
  5.9 7.0 %collective-permute-start.2 = (f32[10,1,4,128]{3,1,2,0:T(1,128)S(1)}, f32[10,1,4,128]{3,1,2,0:T(1,128)S(1)}, u32[]{:S(2)}, u32[]{:S(2)}) collective-permute-start(f32[10,1,4,128]{3,1,2,0:T(1,128)S(1)} %get-tuple-element.16), channel_id=1, source_target_pairs={{0,1},{1,2},{2,3},{3,4},{4,5},{5,6},{6,7},{7,0},{8,9},{9,10},{10,1... | collective-permute-start | bytes 61448 | tf_op jit(solution)/shard_map/ppermute | solution.py:21
  8.1 4.8 %collective-permute-start.3 = (f32[10,1,4,128]{3,1,2,0:T(1,128)S(1)}, f32[10,1,4,128]{3,1,2,0:T(1,128)S(1)}, u32[]{:S(2)}, u32[]{:S(2)}) collective-permute-start(f32[10,1,4,128]{3,1,2,0:T(1,128)S(1)} %get-tuple-element.17), channel_id=1, source_target_pairs={{1,0},{2,1},{3,2},{4,3},{5,4},{6,5},{7,6},{0,7},{9,8},{10,9},{11,1... | collective-permute-start | bytes 61448 | tf_op jit(solution)/shard_map/ppermute | solution.py:24
  13.0 0.7 copy-start.5
  21.0 69.6 %all-to-all-start = ((f32[32,8,5,128]{3,1,2,0:T(8,128)}), f32[32,8,5,128]{3,1,2,0:T(8,128)S(1)}, u32[]{:S(2)}, u32[]{:S(2)}) async-start(f32[32,8,5,128]{3,1,2,0:T(8,128)} %copy.39), calls=%async_computation | async-start | bytes 1310720 | tf_op jit(solution)/shard_map/all_to_all | solution.py:213
  27.6 0.8 copy-start
  90.5 13.2 %all-to-all-start.1 = ((f32[32,8,128]{2,1,0:T(8,128)}), f32[32,8,128]{2,1,0:T(8,128)S(1)}, u32[]{:S(2)}, u32[]{:S(2)}) async-start(f32[32,8,128]{2,1,0:T(8,128)} %bitcast.19), calls=%async_computation.1 | async-start | bytes 262144 | tf_op jit(solution)/shard_map/all_to_all | solution.py:249
  96.1 7.6 %copy-start.1 = (f32[32,8,5,128]{3,2,1,0:T(8,128)}, f32[32,8,5,128]{3,2,1,0:T(8,128)S(1)}, u32[]{:S(2)}) copy-start(f32[32,8,5,128]{3,2,1,0:T(8,128)S(1)} %copy.40) | copy-start | bytes 1966084
  103.7 0.7 copy-start.3

commit v4 on v3

--- a/solution.py
+++ b/solution.py
@@ -149,6 +149,20 @@
     lax.fori_loop(0, tiles, finish, 0, unroll=4)
 
 
+def pack_kernel(tiles, send_ref, packed_ref, note_ref, out_ref):
+    lane = lax.broadcasted_iota(jnp.int32, (1, note_ref.shape[1]), 1)
+    blank = jnp.where(lane == 2, note_ref[0:1, :], 0.0)
+    out_ref[...] = jnp.broadcast_to(blank[None], out_ref.shape)
+
+    def put(t, carry):
+        row = send_ref[t]
+        out_ref[row, 0:4, :] = packed_ref[t]
+        out_ref[row, 4:5, :] = note_ref[pl.ds(t, 1), :]
+        return carry
+
+    lax.fori_loop(0, tiles, put, 0, unroll=8)
+
+
 def place_kernel(tiles, from_ref, state_ref, dens_ref, out_ref):
     def put(s, carry):
         row = from_ref[s]
@@ -204,12 +218,14 @@
     lane = slot_ids[None, :]
     note = jnp.where(lane == 0, pair_work.reshape(-1, 1), 0.0)
     note = jnp.where(lane == 1, (slot_local + 1).astype(jnp.float32)[:, None], note)
-    tile_state = jnp.concatenate(
-        [packed.reshape(tile_total, 4, slot_width), note[:, None, :]], axis=1
-    )
-    send_state = jnp.zeros((send_rows, 5, slot_width), jnp.float32).at[send_index].set(tile_state)
-    mark = jnp.logical_and(jnp.arange(5)[:, None] == 4, lane == 2)
-    send_state = jnp.where(mark[None], local_work, send_state)
+    note = jnp.where(lane == 2, local_work, note)
+    send_state = pl.pallas_call(
+        functools.partial(pack_kernel, tile_total),
+        out_shape=jax.ShapeDtypeStruct((send_rows, 5, slot_width), jnp.float32),
+        in_specs=[SMEM, VMEM, VMEM],
+        out_specs=VMEM,
+        name="pack",
+    )(send_index, packed.reshape(tile_total, 4, slot_width), note)
     recv_state = lax.all_to_all(
         send_state.reshape(device_total, capacity, 5, slot_width),
         ("gx", "gy"),

time: 110 us -> 109 us (level)
  local copies, waits for them, and re-layouts: 11.1 us -> 7.73 us
  other arithmetic: 5.29 us -> 7.19 us
  Pallas kernels: 64.4 us -> 65.8 us
  waiting for transfers between devices: 8.46 us -> 7.27 us
    scatter x1 -> x0, local copies, waits for them, and re-layouts: 4.36 us -> none  [body(): jnp.zeros((send_rows, 5, slot_width), jnp.float32).at[send_index]]
    pallas_call x0 -> x1, Pallas kernels: none -> 2.24 us  [body(): pl.pallas_call(functools.partial(pack_kernel, tile_total), out_shape=jax....]
    reshape x1, local copies, waits for them, and re-layouts: 0.96 us -> 2.2 us  [body(): send_state.reshape(device_total, capacity, 5, slot_width)]
    unnamed x17 -> x19, local copies, waits for them, and re-layouts: 3.88 us -> 3.96 us
  transfers between devices with their start and end apart: 6 -> 6, of which waited for: 4 -> 2; matrix products, arithmetic and copies ran while one was open for 3% -> 4% of each run, Pallas kernels for 57% -> 57%
where the time goes in v4:
time: 109 us; the launch traced here: 108 us
  Pallas kernels  65.8 us (60%)
  starting transfers between devices  19.3 us (18%)
  local copies, waits for them, and re-layouts  7.73 us (7%)
  waiting for transfers between devices  7.27 us (7%)
  other arithmetic  7.19 us (7%)
    pallas_call x1, Pallas kernels, body(): pl.pallas_call(functools.partial(density_kernel, rows_local, cols_local),...  61.3 us
    all_to_all x1, starting transfers between devices, body(): lax.all_to_all(send_state.reshape(device_total, capacity, 5, slot_width),...  6.23 us
    all_to_all x1, waiting for transfers between devices, body(): lax.all_to_all(send_density.reshape(device_total, capacity, slot_width),...  5.65 us
    all_to_all x1, starting transfers between devices, body(): lax.all_to_all(send_density.reshape(device_total, capacity, slot_width),...  5.16 us
    ppermute x2, starting transfers between devices, extended(): lax.ppermute(lax.slice_in_dim(block, 0, width, axis=dim), axis, backward)  5.09 us
    unnamed x19, local copies, waits for them, and re-layouts  3.96 us
    ppermute x2, starting transfers between devices, extended(): lax.ppermute(lax.slice_in_dim(block, block.shape[dim] - width, None, axis...  2.86 us
    pallas_call x1, Pallas kernels, body(): pl.pallas_call(functools.partial(place_kernel, tile_total), out_shape=jax...  2.3 us
  transfers between devices with their start and end apart: 6, of which 2 were waited for; matrix products, arithmetic and copies ran while one was open for 4% of the time, Pallas kernels for 57%

profile of v4, /device:TPU:0, one launch (start us, length us, event | category | flops | bytes accessed | tf_op | source)
XLA Modules:
  0.0 108.2 jit_solution(14576290454822329593)
XLA Ops:
  0.6 1.0 select_bitcast_fusion
  1.6 0.5 collective-permute-start
  2.2 2.0 %collective-permute-start.1 = (f32[1,16,4,128]{3,1,2,0:T(8,128)S(1)}, f32[1,16,4,128]{3,1,2,0:T(8,128)S(1)}, u32[]{:S(2)}, u32[]{:S(2)}) collective-permute-start(f32[1,16,4,128]{3,1,2,0:T(8,128)S(1)} %get-tuple-element.15), channel_id=1, source_target_pairs={{8,0},{16,8},{24,16},{0,24},{9,1},{17,9},{25,17},{1,25},{10,2},{18... | collective-permute-start | bytes 98312 | tf_op jit(solution)/shard_map/ppermute | solution.py:24
  5.1 0.8 pad_maximum_fusion.1.packed_ref
  6.0 2.3 %collective-permute-start.2 = (f32[10,1,4,128]{3,1,2,0:T(1,128)S(1)}, f32[10,1,4,128]{3,1,2,0:T(1,128)S(1)}, u32[]{:S(2)}, u32[]{:S(2)}) collective-permute-start(f32[10,1,4,128]{3,1,2,0:T(1,128)S(1)} %get-tuple-element.12), channel_id=1, source_target_pairs={{0,1},{1,2},{2,3},{3,4},{4,5},{5,6},{6,7},{7,0},{8,9},{9,10},{10,1... | collective-permute-start | bytes 61448 | tf_op jit(solution)/shard_map/ppermute | solution.py:21
  8.3 3.1 %collective-permute-start.3 = (f32[10,1,4,128]{3,1,2,0:T(1,128)S(1)}, f32[10,1,4,128]{3,1,2,0:T(1,128)S(1)}, u32[]{:S(2)}, u32[]{:S(2)}) collective-permute-start(f32[10,1,4,128]{3,1,2,0:T(1,128)S(1)} %get-tuple-element.13), channel_id=1, source_target_pairs={{1,0},{2,1},{3,2},{4,3},{5,4},{6,5},{7,6},{0,7},{9,8},{10,9},{11,1... | collective-permute-start | bytes 61448 | tf_op jit(solution)/shard_map/ppermute | solution.py:24
  11.5 1.6 %collective-permute-done.2 = f32[10,1,4,128]{3,1,2,0:T(1,128)S(1)} collective-permute-done((f32[10,1,4,128]{3,1,2,0:T(1,128)S(1)}, f32[10,1,4,128]{3,1,2,0:T(1,128)S(1)}, u32[]{:S(2)}, u32[]{:S(2)}) %collective-permute-start.2) | collective-permute-done | bytes 20512 | tf_op jit(solution)/shard_map/ppermute | solution.py:21
  13.3 0.6 copy-done.6
  13.9 0.8 fusion.23
  14.7 1.4 %select_select_fusion.note_ref = f32[128,128]{1,0:T(8,128)} fusion(f32[128]{0:T(128)S(1)} %broadcast_in_dim.95, f32[128]{0:T(128)S(1)} %convert_element_type.36, f32[]{:T(128)} %get-tuple-element.10, pred[128]{0:T(512)(128)(4,1)S(1)} %get-tuple-element.20, pred[128]{0:T(512)(128)(4,1)S(1)} %get-tuple-element.21, pred[128]{0:T(512)(128)(4,1)S(1)} %iota_compare_fusion.5), kind=kLoop, calls=%fused_computation.11 | loop fusion | flops 49152 | bytes 66948 | tf_op jit(solution)/shard_map/jit(_where)/select_n | solution.py:221
  16.1 2.2 %pack.1 = f32[256,5,128]{2,1,0:T(8,128)} custom-call(s32[128]{0:T(128)} %multiply_add_fusion.send_ref, f32[128,4,128]{2,1,0:T(4,128)} %pad_maximum_fusion.1.packed_ref, f32[128,128]{1,0:T(8,128)} %select_select_fusion.note_ref), custom_call_target="tpu_custom_call" | custom-call | tf_op jit(solution)/shard_map/pack/pallas_call | solution.py:222
  18.4 2.2 %copy.30 = f32[32,8,5,128]{3,1,2,0:T(8,128)} copy(f32[32,8,5,128]{3,2,1,0:T(8,128)} %bitcast.59) | data formatting | bytes 1310720 | tf_op jit(solution)/shard_map/reshape | solution.py:230
  20.6 6.2 %all-to-all-start = ((f32[32,8,5,128]{3,1,2,0:T(8,128)}), f32[32,8,5,128]{3,1,2,0:T(8,128)S(1)}, u32[]{:S(2)}, u32[]{:S(2)}) async-start(f32[32,8,5,128]{3,1,2,0:T(8,128)} %copy.30), calls=%async_computation | async-start | bytes 1310720 | tf_op jit(solution)/shard_map/all_to_all | solution.py:229
  27.1 0.7 copy-done.1
  27.8 61.3 %density.1 = f32[256,128]{1,0:T(8,128)} custom-call(s32[1024]{0:T(1024)S(1)} %reshape.87.pair_ref, s32[128]{0:T(128)S(1)} %copy-done, f32[180,4,128]{2,1,0:T(4,128)S(1)} %bitcast.55, f32[128,128]{1,0:T(8,128)S(1)} %bitcast.56), custom_call_target="tpu_custom_call" | custom-call | flops 377487360 | bytes 188743680 | tf_op jit(solution)/shard_map/density/pallas_call | solution.py:238
  89.1 5.2 %all-to-all-start.1 = ((f32[32,8,128]{2,1,0:T(8,128)}), f32[32,8,128]{2,1,0:T(8,128)S(1)}, u32[]{:S(2)}, u32[]{:S(2)}) async-start(f32[32,8,128]{2,1,0:T(8,128)} %bitcast.17), calls=%async_computation.1 | async-start | bytes 262144 | tf_op jit(solution)/shard_map/all_to_all | solution.py:265
  94.9 0.6 select_reduce_fusion.1.from_ref
  95.7 0.7 slice_reduce_fusion.1
  96.4 5.7 %all-to-all-done.1 = f32[32,8,128]{2,1,0:T(8,128)S(1)} async-done(((f32[32,8,128]{2,1,0:T(8,128)}), f32[32,8,128]{2,1,0:T(8,128)S(1)}, u32[]{:S(2)}, u32[]{:S(2)}) %all-to-all-start.1) | async-done | bytes 131104 | tf_op jit(solution)/shard_map/all_to_all | solution.py:265
  102.1 0.7 copy-done.4
  102.7 2.3 %place.1 = f32[128,5,128]{2,1,0:T(8,128)} custom-call(s32[128]{0:T(128)} %select_reduce_fusion.1.from_ref, f32[256,5,128]{2,1,0:T(8,128)} %bitcast.58, f32[256,128]{1,0:T(8,128)} %bitcast.65), custom_call_target="tpu_custom_call" | custom-call | tf_op jit(solution)/shard_map/place/pallas_call | solution.py:282
  105.0 1.8 %copy.34 = f32[8,16,5,128]{3,1,2,0:T(8,128)} copy(f32[8,16,5,128]{3,2,1,0:T(8,128)} %bitcast.60) | data formatting | bytes 655360
  106.9 0.6 multiply_divide_fusion
  107.5 0.7 div.56
  (39 shorter events, 2.4 us)
Async XLA Ops:
  0.6 1.0 copy-start.3
  1.6 4.3 %collective-permute-start = (f32[1,16,4,128]{3,1,2,0:T(8,128)S(1)}, f32[1,16,4,128]{3,1,2,0:T(8,128)S(1)}, u32[]{:S(2)}, u32[]{:S(2)}) collective-permute-start(f32[1,16,4,128]{3,1,2,0:T(8,128)S(1)} %get-tuple-element.14), channel_id=1, source_target_pairs={{0,8},{8,16},{16,24},{24,0},{1,9},{9,17},{17,25},{25,1},{2,10},{10... | collective-permute-start | bytes 98312 | tf_op jit(solution)/shard_map/ppermute | solution.py:21
  2.2 2.1 %copy-start.7 = (s32[8,16]{1,0:T(8,128)S(1)}, s32[8,16]{1,0:T(8,128)}, u32[]{:S(2)}) copy-start(s32[8,16]{1,0:T(8,128)} %param.11) | copy-start | bytes 1540
  2.2 3.8 %collective-permute-start.1 = (f32[1,16,4,128]{3,1,2,0:T(8,128)S(1)}, f32[1,16,4,128]{3,1,2,0:T(8,128)S(1)}, u32[]{:S(2)}, u32[]{:S(2)}) collective-permute-start(f32[1,16,4,128]{3,1,2,0:T(8,128)S(1)} %get-tuple-element.15), channel_id=1, source_target_pairs={{8,0},{16,8},{24,16},{0,24},{9,1},{17,9},{25,17},{1,25},{10,2},{18... | collective-permute-start | bytes 98312 | tf_op jit(solution)/shard_map/ppermute | solution.py:24
  4.2 0.9 copy-start.5
  6.0 7.1 %collective-permute-start.2 = (f32[10,1,4,128]{3,1,2,0:T(1,128)S(1)}, f32[10,1,4,128]{3,1,2,0:T(1,128)S(1)}, u32[]{:S(2)}, u32[]{:S(2)}) collective-permute-start(f32[10,1,4,128]{3,1,2,0:T(1,128)S(1)} %get-tuple-element.12), channel_id=1, source_target_pairs={{0,1},{1,2},{2,3},{3,4},{4,5},{5,6},{6,7},{7,0},{8,9},{9,10},{10,1... | collective-permute-start | bytes 61448 | tf_op jit(solution)/shard_map/ppermute | solution.py:21
  8.3 4.8 %collective-permute-start.3 = (f32[10,1,4,128]{3,1,2,0:T(1,128)S(1)}, f32[10,1,4,128]{3,1,2,0:T(1,128)S(1)}, u32[]{:S(2)}, u32[]{:S(2)}) collective-permute-start(f32[10,1,4,128]{3,1,2,0:T(1,128)S(1)} %get-tuple-element.13), channel_id=1, source_target_pairs={{1,0},{2,1},{3,2},{4,3},{5,4},{6,5},{7,6},{0,7},{9,8},{10,9},{11,1... | collective-permute-start | bytes 61448 | tf_op jit(solution)/shard_map/ppermute | solution.py:24
  13.2 0.7 copy-start.6
  20.6 68.5 %all-to-all-start = ((f32[32,8,5,128]{3,1,2,0:T(8,128)}), f32[32,8,5,128]{3,1,2,0:T(8,128)S(1)}, u32[]{:S(2)}, u32[]{:S(2)}) async-start(f32[32,8,5,128]{3,1,2,0:T(8,128)} %copy.30), calls=%async_computation | async-start | bytes 1310720 | tf_op jit(solution)/shard_map/all_to_all | solution.py:229
  27.0 0.8 copy-start.1
  27.1 0.7 copy-start
  89.1 13.0 %all-to-all-start.1 = ((f32[32,8,128]{2,1,0:T(8,128)}), f32[32,8,128]{2,1,0:T(8,128)S(1)}, u32[]{:S(2)}, u32[]{:S(2)}) async-start(f32[32,8,128]{2,1,0:T(8,128)} %bitcast.17), calls=%async_computation.1 | async-start | bytes 262144 | tf_op jit(solution)/shard_map/all_to_all | solution.py:265
  94.5 7.6 %copy-start.2 = (f32[32,8,5,128]{3,2,1,0:T(8,128)}, f32[32,8,5,128]{3,2,1,0:T(8,128)S(1)}, u32[]{:S(2)}) copy-start(f32[32,8,5,128]{3,2,1,0:T(8,128)S(1)} %copy.31) | copy-start | bytes 1966084
  102.1 0.7 copy-start.4
